TPU v7x, 512 devices: a whole 4x8x8 slice. The times are simulated.
512 devices in a mesh: rows: 16 (over z, core), centres: 32 (over x, y).
Axes of the slice: x: 4, y: 8, z: 8, core: 2. Of those that a mesh axis runs over, the one named last changes fastest.
Arguments:
- features: bfloat16 [16384, 256], P('rows', 'centres'), may hold values from -11 to 11
- targets: bfloat16 [16384, 128], P('rows'), may hold values from -6 to 6
- centre_points: bfloat16 [16384, 256], P('centres'), may hold values from -11 to 11
- precond: bfloat16 [16384, 512], P('centres'), as said below
Outputs:
- coefficients: float32 [16384, 128], P('centres')
- fitted: float32 [16384, 128], P('rows')
Inputs may be any that keep to these rules, and one draw needn't show every extreme that they name: Each diagonal block of 512 x 512 entries of precond is symmetric positive definite.
All inputs are finite; a program needn't handle non-finite values.
Results may differ from a plain program's by a relative error of at most 0.0076.
Values may be sent and summed in bfloat16 or wider, within the bound.
No kernel may reach another device: no remote copies, remote signals or barrier semaphores. Data moves between devices by JAX's collectives and lax.ppermute only.
A program may use at most 64 MiB of HBM per device.

v0:
```python
import jax
import jax.numpy as jnp
from jax import lax
from jax.sharding import PartitionSpec as P

ITERS = 2


RIDGE_WEIGHT = 0.02


def copy_for_each(value, axis):
    copies = jnp.broadcast_to(value, (lax.axis_size(axis), *value.shape))
    return lax.all_to_all(copies, axis, split_axis=0, concat_axis=0, tiled=True)


def joined_along(tiles, dim):
    shape = list(tiles.shape[1:])
    shape[dim] *= tiles.shape[0]
    return jnp.moveaxis(tiles, 0, dim).reshape(shape)


def gathered_copies(value, axis, dim):
    tiles = copy_for_each(value, axis)
    return joined_along(tiles, dim)


def in_blocks(value, dim, size):
    shape = value.shape
    tiles = value.reshape(*shape[:dim], size, shape[dim] // size, *shape[dim + 1 :])
    return jnp.moveaxis(tiles, dim, 0)


def summed_on_arrival(value, axis, dim):
    tiles = in_blocks(value, dim, lax.axis_size(axis))
    arrived = lax.all_to_all(tiles, axis, split_axis=0, concat_axis=0, tiled=True)
    return arrived.sum(axis=0)


def of_everyone(value, axis):
    everything = copy_for_each(value, axis)
    return jnp.sum(everything, axis=0)


def packed_total(arrays, axis):
    ravelled, at, gathered = (jnp.concatenate([a.reshape(-1) for a in arrays]), 0, [])
    so_far = of_everyone(ravelled, axis)
    for a in arrays:
        gathered.append(so_far[at : at + a.size].reshape(a.shape))
        at += a.size
    return tuple(gathered)


def over_pieces(value, axis):
    return lax.all_gather(value, axis).sum(0)


def per_device(features, targets, centre_points, precond):
    rows_here = features.shape[0]
    group_rows = float(rows_here)
    gathered = gathered_copies(features, "centres", 1)
    feature_count = gathered.shape[1]
    inner_products = jnp.einsum(
        "rd,cd->rc", gathered, centre_points, preferred_element_type=jnp.float32
    )
    gathered_float = gathered.astype(jnp.float32)
    centre_float = centre_points.astype(jnp.float32)
    row_scale = 1.0 / jnp.sqrt(jnp.mean(gathered_float * gathered_float, axis=1) + 1e-06)
    centre_scale = 1.0 / jnp.sqrt(jnp.mean(centre_float * centre_float, axis=1) + 1e-06)
    cosine = (
        inner_products * row_scale[:, None] * centre_scale[None, :] / jnp.float32(feature_count)
    )
    kernel = jnp.exp(8.0 * (cosine - 1.0)).astype(jnp.bfloat16)

    def transposed(values, divisor):
        return jnp.einsum("rc,rt->ct", kernel, values, preferred_element_type=jnp.float32) / divisor

    def precondition(residual):
        return jnp.dot(precond, residual.astype(jnp.bfloat16), preferred_element_type=jnp.float32)

    def stats_merged(residual, scaled, direction):
        return packed_total(
            (
                jnp.sum(residual * scaled, axis=0),
                jnp.sum(scaled * scaled, axis=0),
                jnp.sum(scaled * direction, axis=0),
            ),
            "centres",
        )

    rhs = over_pieces(transposed(targets, jnp.sqrt(jnp.float32(group_rows))), "rows")
    coefficients = jnp.zeros_like(rhs)
    fitted = jnp.zeros((), jnp.float32)
    residual = rhs
    scaled = precondition(residual)
    direction = scaled
    product_now, direction_sq, unused_term = stats_merged(residual, scaled, scaled)
    for iteration in range(ITERS):
        narrow = direction.astype(jnp.bfloat16)
        segment = summed_on_arrival(
            jnp.dot(kernel, narrow, preferred_element_type=jnp.float32), "centres", 0
        )
        segment, rounded = (segment, gathered_copies(segment.astype(jnp.bfloat16), "centres", 0))
        rounded_float = rounded.astype(jnp.float32)
        column_part, output_sq = (
            over_pieces(transposed(rounded, group_rows), "rows"),
            over_pieces(jnp.sum(rounded_float * rounded_float, axis=0) / group_rows, "rows"),
        )
        applied = column_part + RIDGE_WEIGHT * direction
        step_size = product_now / (output_sq + RIDGE_WEIGHT * direction_sq)
        coefficients = coefficients + step_size * direction
        fitted = fitted + step_size * segment
        residual = residual - step_size * applied
        if iteration + 1 < ITERS:
            scaled = precondition(residual)
            product_next, scaled_sq, cross_term = stats_merged(residual, scaled, direction)
            momentum = product_next / product_now
            direction_sq = (
                scaled_sq + 2.0 * momentum * cross_term + momentum * momentum * direction_sq
            )
            direction = scaled + momentum * direction
            product_now = product_next
    fitted = gathered_copies(fitted, "centres", 0)
    return (coefficients, fitted)


def solution(mesh):
    return jax.shard_map(
        per_device,
        mesh=mesh,
        in_specs=(P("rows", "centres"), P("rows", None), P("centres", None), P("centres", None)),
        out_specs=(P("centres", None), P("rows", None)),
        check_vma=False,
    )
```

profile of v0, /device:TPU:1, one launch (start us, length us, event | category | flops | bytes accessed | tf_op | source)
XLA Modules:
  0.0 274.9 jit_solution(6259399301810072808)
XLA Ops:
  7.2 1.6 broadcast_in_dim.12
  8.8 10.5 %all-to-all-start = ((bf16[32,1024,8]{1,2,0:T(8,128)(2,1)}), bf16[32,1024,8]{1,2,0:T(8,128)(2,1)S(1)}, u32[]{:S(2)}, u32[]{:S(2)}) async-start(bf16[32,1024,8]{1,2,0:T(8,128)(2,1)} %broadcast_in_dim.12), calls=%async_computation | async-start | bytes 1048576 | tf_op jit(solution)/shard_map/all_to_all | solution.py:14
  19.4 1.1 multiply_reduce_fusion.3
  20.5 13.4 %all-to-all-done = bf16[32,1024,8]{1,2,0:T(8,128)(2,1)S(1)} async-done(((bf16[32,1024,8]{1,2,0:T(8,128)(2,1)}), bf16[32,1024,8]{1,2,0:T(8,128)(2,1)S(1)}, u32[]{:S(2)}, u32[]{:S(2)}) %all-to-all-start) | async-done | bytes 524320 | tf_op jit(solution)/shard_map/all_to_all | solution.py:14
  34.0 0.9 exponential_convert_fusion
  35.0 1.2 convolution_multiply_fusion.1
  36.2 48.4 %all-gather.9.cloned.1.call-done = f32[8192,128]{1,0:T(8,128)} async-done(((f32[512,128]{1,0:T(8,128)}), f32[8192,128]{1,0:T(8,128)}) %all-gather.9.cloned.1.call-update) | async-done | bytes 4194320 | tf_op jit(solution)/shard_map/all_gather | solution.py:55
  84.6 2.4 reduce_sum.159
  87.0 0.1 copy.17
  87.2 0.4 multiply_reduce_fusion.8
  87.6 0.4 fusion.4
  88.0 23.1 %all_to_all.42 = f32[32,32,128]{2,1,0:T(8,128)S(1)} all-to-all(f32[32,32,128]{2,1,0:T(8,128)S(1)} %bitcast.33), channel_id=1, replica_groups=mesh['rows'=16,'centres'=32] {'centres'}, dimensions={0} | all-to-all | bytes 1048576 | tf_op jit(solution)/shard_map/all_to_all | solution.py:36
  111.2 17.7 %all_to_all.43 = bf16[32,32,128]{2,1,0:T(8,128)(2,1)S(1)} all-to-all(bf16[32,32,128]{2,1,0:T(8,128)(2,1)S(1)} %broadcast_in_dim.28), channel_id=1, replica_groups=mesh['rows'=16,'centres'=32] {'centres'}, dimensions={0} | all-to-all | bytes 524288 | tf_op jit(solution)/shard_map/all_to_all | solution.py:14
  128.9 1.2 convolution_multiply_fusion
  130.2 14.8 %all_to_all.44 = f32[32,1,384]{2,1,0:T(1,128)S(1)} all-to-all(f32[32,1,384]{2,1,0:T(1,128)S(1)} %broadcast_in_dim.13), channel_id=1, replica_groups=mesh['rows'=16,'centres'=32] {'centres'}, dimensions={0} | all-to-all | bytes 98304 | tf_op jit(solution)/shard_map/all_to_all | solution.py:14
  145.1 0.2 multiply_reduce_fusion.2
  145.2 19.1 %all-gather.4 = f32[16,1,128]{2,1,0:T(1,128)S(1)} all-gather(f32[1,1,128]{2,1,0:T(1,128)S(1)} %multiply_bitcast_fusion.1), channel_id=3, replica_groups=mesh['rows'=16,'centres'=32] {'rows'}, dimensions={0}, use_global_device_ids=true | all-gather | bytes 8704 | tf_op jit(solution)/shard_map/all_gather | solution.py:55
  164.4 7.6 %all-gather.11.cloned.1.call-done = f32[8192,128]{1,0:T(8,128)} async-done(((f32[512,128]{1,0:T(8,128)}), f32[8192,128]{1,0:T(8,128)}) %all-gather.11.cloned.1.call-update) | async-done | bytes 4194320 | tf_op jit(solution)/shard_map/all_gather | solution.py:55
  172.0 2.4 reduce_sum.166
  174.4 0.1 copy.19
  174.5 0.5 multiply_reduce_fusion.6
  175.0 17.8 %all_to_all.45 = f32[32,1,384]{2,1,0:T(1,128)S(1)} all-to-all(f32[32,1,384]{2,1,0:T(1,128)S(1)} %broadcast_in_dim.29), channel_id=1, replica_groups=mesh['rows'=16,'centres'=32] {'centres'}, dimensions={0} | all-to-all | bytes 98304 | tf_op jit(solution)/shard_map/all_to_all | solution.py:14
  192.9 0.5 fusion.1
  193.4 16.7 %all_to_all.46 = f32[32,32,128]{2,1,0:T(8,128)S(1)} all-to-all(f32[32,32,128]{2,1,0:T(8,128)S(1)} %bitcast.32), channel_id=1, replica_groups=mesh['rows'=16,'centres'=32] {'centres'}, dimensions={0} | all-to-all | bytes 1048576 | tf_op jit(solution)/shard_map/all_to_all | solution.py:36
  210.2 17.4 %all_to_all.47 = bf16[32,32,128]{2,1,0:T(8,128)(2,1)S(1)} all-to-all(bf16[32,32,128]{2,1,0:T(8,128)(2,1)S(1)} %broadcast_in_dim.30), channel_id=1, replica_groups=mesh['rows'=16,'centres'=32] {'centres'}, dimensions={0} | all-to-all | bytes 524288 | tf_op jit(solution)/shard_map/all_to_all | solution.py:14
  227.6 0.2 multiply_reduce_fusion.1
  227.8 19.7 %all-gather.5 = f32[16,1,128]{2,1,0:T(1,128)S(1)} all-gather(f32[1,1,128]{2,1,0:T(1,128)S(1)} %multiply_bitcast_fusion), channel_id=5, replica_groups=mesh['rows'=16,'centres'=32] {'rows'}, dimensions={0}, use_global_device_ids=true | all-gather | bytes 8704 | tf_op jit(solution)/shard_map/all_gather | solution.py:55
  247.6 0.9 broadcast_in_dim.31
  248.4 4.2 %all-to-all-start.7 = ((f32[32,32,128]{2,1,0:T(8,128)}), f32[32,32,128]{2,1,0:T(8,128)S(1)}, u32[]{:S(2)}, u32[]{:S(2)}) async-start(f32[32,32,128]{2,1,0:T(8,128)} %broadcast_in_dim.31), calls=%async_computation.7 | async-start | bytes 1048576 | tf_op jit(solution)/shard_map/all_to_all | solution.py:14
  252.8 0.8 copy.22
  253.6 13.7 %all-to-all-done.7 = f32[32,32,128]{2,1,0:T(8,128)S(1)} async-done(((f32[32,32,128]{2,1,0:T(8,128)}), f32[32,32,128]{2,1,0:T(8,128)S(1)}, u32[]{:S(2)}, u32[]{:S(2)}) %all-to-all-start.7) | async-done | bytes 524320 | tf_op jit(solution)/shard_map/all_to_all | solution.py:14
  267.3 0.8 copy.31
  (34 shorter events, 0.9 us)
Async XLA Ops:
  7.2 80.0 %copy-start = (bf16[512,512]{1,0:T(8,128)(2,1)S(1)}, bf16[512,512]{1,0:T(8,128)(2,1)}, u32[]{:S(2)}) copy-start(bf16[512,512]{1,0:T(8,128)(2,1)} %param.7) | copy-start | bytes 1572868
  7.2 26.8 %copy-start.1 = (bf16[512,256]{1,0:T(8,128)(2,1)S(1)}, bf16[512,256]{1,0:T(8,128)(2,1)}, u32[]{:S(2)}) copy-start(bf16[512,256]{1,0:T(8,128)(2,1)} %param.6) | copy-start | bytes 786436
  8.8 25.0 %all-to-all-start = ((bf16[32,1024,8]{1,2,0:T(8,128)(2,1)}), bf16[32,1024,8]{1,2,0:T(8,128)(2,1)S(1)}, u32[]{:S(2)}, u32[]{:S(2)}) async-start(bf16[32,1024,8]{1,2,0:T(8,128)(2,1)} %broadcast_in_dim.12), calls=%async_computation | async-start | bytes 1048576 | tf_op jit(solution)/shard_map/all_to_all | solution.py:14
  19.3 65.3 %all-gather.9.cloned.1.call-start = ((), (), s32[]{:S(2)}) async-start(), calls=%async_computation.8 | async-start | bytes 4456448 | tf_op jit(solution)/shard_map/all_gather | solution.py:55
  34.0 1.0 copy-start.2
  36.2 135.8 %all-gather.11.cloned.1.call-start = ((), (), s32[]{:S(2)}) async-start(), calls=%async_computation.9 | async-start | bytes 4456448 | tf_op jit(solution)/shard_map/all_gather | solution.py:55
  248.4 18.9 %all-to-all-start.7 = ((f32[32,32,128]{2,1,0:T(8,128)}), f32[32,32,128]{2,1,0:T(8,128)S(1)}, u32[]{:S(2)}, u32[]{:S(2)}) async-start(f32[32,32,128]{2,1,0:T(8,128)} %broadcast_in_dim.31), calls=%async_computation.7 | async-start | bytes 1048576 | tf_op jit(solution)/shard_map/all_to_all | solution.py:14
Sparse Core Ops, SparseCore 0:
  36.3 48.3 all-gather.8
  130.2 41.7 all-gather.10
where the time goes:
time: 278 us; the launch traced here: 275 us
  blocking collectives  146 us (53%)
  waiting for transfers between devices  83.1 us (30%)
  starting transfers between devices  14.8 us (5%)
  between operations  14.2 us (5%)
  other arithmetic  6.84 us (2%)
  matrix products  5.03 us (2%)
  local copies, waits for them, and re-layouts  4.59 us (2%)
    all_to_all x4, blocking collectives, copy_for_each(): return lax.all_to_all(copies, axis, split_axis=0, concat_axis=0, tiled=True)  67.7 us
    all_gather x2, waiting for transfers between devices, over_pieces(): return lax.all_gather(value, axis).sum(0)  56 us
    all_to_all x2, blocking collectives, summed_on_arrival(): lax.all_to_all(tiles, axis, split_axis=0, concat_axis=0, tiled=True)  39.8 us
    all_gather x2, blocking collectives, over_pieces(): return lax.all_gather(value, axis).sum(0)  38.9 us
    all_to_all x2, waiting for transfers between devices, copy_for_each(): return lax.all_to_all(copies, axis, split_axis=0, concat_axis=0, tiled=True)  27.1 us
    all_to_all x2, starting transfers between devices, copy_for_each(): return lax.all_to_all(copies, axis, split_axis=0, concat_axis=0, tiled=True)  14.7 us
  transfers between devices with their start and end apart: 4, of which 4 were waited for; matrix products, arithmetic and copies ran while one was open for 1% of the time, Pallas kernels for 0%

commit v1 on v0

v1 whole, which is shorter than its diff:
```python
import jax
import jax.numpy as jnp
from jax import lax
from jax.sharding import PartitionSpec as P

RIDGE_WEIGHT = 0.02


def exchanged(tiles, axis):
    return lax.all_to_all(tiles, axis, split_axis=0, concat_axis=0, tiled=True)


def copies_of(value, axis):
    copies = jnp.broadcast_to(value, (lax.axis_size(axis), *value.shape))
    return exchanged(copies, axis)


def two_halves(rows):
    high = rows.astype(jnp.bfloat16)
    low = (rows - high.astype(jnp.float32)).astype(jnp.bfloat16)
    return high, low


def extra_rows(sums):
    parts = [p[None, :] for s in sums for p in two_halves(s)]
    width = sums[0].shape[0]
    parts.append(jnp.zeros((8 - len(parts), width), jnp.bfloat16))
    return jnp.concatenate(parts, axis=0)


def summed_shares(partial, sums, axis):
    size = lax.axis_size(axis)
    share = partial.shape[0] // size
    tiles = partial.astype(jnp.bfloat16).reshape(size, share, partial.shape[1])
    if sums:
        rows = extra_rows(sums)
        tiles = jnp.concatenate(
            [tiles, jnp.broadcast_to(rows, (size, *rows.shape))], axis=1
        )
    arrived = exchanged(tiles, axis).astype(jnp.float32).sum(axis=0)
    totals = [arrived[share + 2 * i] + arrived[share + 2 * i + 1] for i in range(len(sums))]
    return arrived[:share], totals


def per_device(features, targets, centre_points, precond):
    group_rows = float(features.shape[0])
    gathered = copies_of(features.T, "centres").reshape(-1, features.shape[0])
    feature_count = gathered.shape[0]
    gathered_float = gathered.astype(jnp.float32)
    centre_float = centre_points.astype(jnp.float32)
    row_scale = 1.0 / jnp.sqrt(jnp.mean(gathered_float * gathered_float, axis=0) + 1e-06)
    centre_scale = 1.0 / jnp.sqrt(jnp.mean(centre_float * centre_float, axis=1) + 1e-06)
    inner_products = jnp.dot(centre_points, gathered, preferred_element_type=jnp.float32)
    cosine = (
        inner_products * row_scale[None, :] * centre_scale[:, None] / jnp.float32(feature_count)
    )
    kernel = jnp.exp(8.0 * (cosine - 1.0)).astype(jnp.bfloat16)

    def transposed(values):
        return jnp.dot(kernel, values, preferred_element_type=jnp.float32)

    def forward(values):
        return jnp.einsum(
            "cr,ct->rt", kernel, values.astype(jnp.bfloat16), preferred_element_type=jnp.float32
        )

    def precondition(residual):
        return jnp.dot(precond, residual, preferred_element_type=jnp.float32)

    def whole(share, axis):
        return copies_of(share.astype(jnp.bfloat16), axis).reshape(-1, share.shape[1])

    def column_sum(a, b):
        return jnp.sum(a * b, axis=0)

    position = lax.axis_index("rows")
    residual_share, _ = summed_shares(
        transposed(targets) / jnp.sqrt(jnp.float32(group_rows)), [], "rows"
    )
    residual = whole(residual_share, "rows")
    direction = precondition(residual)
    sums = [
        column_sum(residual.astype(jnp.float32), direction),
        column_sum(direction, direction),
    ]
    rows_share, (product_now, direction_sq) = summed_shares(forward(direction), sums, "centres")
    rounded = whole(rows_share, "centres")
    rounded_float = rounded.astype(jnp.float32)
    column_share, (rows_sq,) = summed_shares(
        transposed(rounded) / group_rows, [column_sum(rounded_float, rounded_float)], "rows"
    )
    share = column_share.shape[0]
    direction_share = lax.dynamic_slice_in_dim(direction, position * share, share, 0)
    step_size = product_now / (rows_sq / group_rows + RIDGE_WEIGHT * direction_sq)
    residual_share = residual_share - step_size * (column_share + RIDGE_WEIGHT * direction_share)
    residual = whole(residual_share, "rows")
    scaled = precondition(residual)
    sums = [
        column_sum(residual.astype(jnp.float32), scaled),
        column_sum(scaled, scaled),
        column_sum(scaled, direction),
    ]
    scaled_rows_share, (product_next, scaled_sq, cross_term) = summed_shares(
        forward(scaled), sums, "centres"
    )
    momentum = product_next / product_now
    next_sq = scaled_sq + 2.0 * momentum * cross_term + momentum * momentum * direction_sq
    next_direction = scaled + momentum * direction
    next_rows_share = scaled_rows_share + momentum * rows_share
    next_rows = whole(next_rows_share, "centres").astype(jnp.float32)
    rows_sq = jnp.sum(copies_of(column_sum(next_rows, next_rows)[None], "rows"), axis=(0, 1))
    next_step = product_next / (rows_sq / group_rows + RIDGE_WEIGHT * next_sq)
    coefficients = step_size * direction + next_step * next_direction
    fitted = step_size * rounded_float + next_step * next_rows
    return (coefficients, fitted)


def solution(mesh):
    return jax.shard_map(
        per_device,
        mesh=mesh,
        in_specs=(P("rows", "centres"), P("rows", None), P("centres", None), P("centres", None)),
        out_specs=(P("centres", None), P("rows", None)),
        check_vma=False,
    )
```

time: 278 us -> 176 us (0.63)
  waiting for transfers between devices: 83.1 us -> 33.4 us
  blocking collectives: 146 us -> 107 us
  between operations: 14.2 us -> 0.93 us
  starting transfers between devices: 14.8 us -> 24.3 us
  other arithmetic: 6.84 us -> 2.72 us
    all_gather x2 -> x0, waiting for transfers between devices: 56 us -> none  [over_pieces(): return lax.all_gather(value, axis).sum(0)]
    all_gather x2 -> x0, blocking collectives: 38.9 us -> none  [over_pieces(): return lax.all_gather(value, axis).sum(0)]
    all_to_all x2 -> x3, starting transfers between devices: 14.7 us -> 24.3 us  [exchanged(): return lax.all_to_all(tiles, axis, split_axis=0, concat_axis=0, tiled=True)]
    all_to_all x2 -> x3, waiting for transfers between devices: 27.1 us -> 33.4 us  [exchanged(): return lax.all_to_all(tiles, axis, split_axis=0, concat_axis=0, tiled=True)]
    reduce_sum x11 -> x8, other arithmetic: 5.52 us -> 0.61 us  [the longest x2 0.3 us: column_sum(): return jnp.sum(a * b, axis=0)]
    all_to_all x6 -> x7, blocking collectives: 107 us -> 107 us  [exchanged(): return lax.all_to_all(tiles, axis, split_axis=0, concat_axis=0, tiled=True)]
  transfers between devices with their start and end apart: 4 -> 3, of which waited for: 4 -> 3; matrix products, arithmetic and copies ran while one was open for 1% -> 0% of each run, Pallas kernels for 0% -> 0%
where the time goes in v1:
time: 176 us
  blocking collectives  107 us (61%)
  waiting for transfers between devices  33.4 us (19%)
  starting transfers between devices  24.3 us (14%)
  local copies, waits for them, and re-layouts  4.12 us (2%)
  matrix products  3.37 us (2%)
  other arithmetic  2.72 us (2%)
    all_to_all x7, blocking collectives, exchanged(): return lax.all_to_all(tiles, axis, split_axis=0, concat_axis=0, tiled=True)  107 us
    all_to_all x3, waiting for transfers between devices, exchanged(): return lax.all_to_all(tiles, axis, split_axis=0, concat_axis=0, tiled=True)  33.4 us
    all_to_all x3, starting transfers between devices, exchanged(): return lax.all_to_all(tiles, axis, split_axis=0, concat_axis=0, tiled=True)  24.3 us
  transfers between devices with their start and end apart: 3, of which 3 were waited for; matrix products, arithmetic and copies ran while one was open for 0% of the time, Pallas kernels for 0%

profile of v1, /device:TPU:1, one launch (start us, length us, event | category | flops | bytes accessed | tf_op | source)
XLA Modules:
  0.0 175.7 jit_solution(18126237784095064378)
XLA Ops:
  0.7 1.6 broadcast_in_dim.24
  2.3 10.5 %all-to-all-start = ((bf16[32,8,1024]{2,1,0:T(8,128)(2,1)}), bf16[32,8,1024]{2,1,0:T(8,128)(2,1)S(1)}, u32[]{:S(2)}, u32[]{:S(2)}) async-start(bf16[32,8,1024]{2,1,0:T(8,128)(2,1)} %broadcast_in_dim.24), calls=%async_computation | async-start | bytes 1048576 | tf_op jit(solution)/shard_map/all_to_all | solution.py:10
  12.8 0.1 multiply_reduce_fusion.3
  13.0 14.4 %all-to-all-done = bf16[32,8,1024]{2,1,0:T(8,128)(2,1)S(1)} async-done(((bf16[32,8,1024]{2,1,0:T(8,128)(2,1)}), bf16[32,8,1024]{2,1,0:T(8,128)(2,1)S(1)}, u32[]{:S(2)}, u32[]{:S(2)}) %all-to-all-start) | async-done | bytes 524320 | tf_op jit(solution)/shard_map/all_to_all | solution.py:10
  27.3 0.1 multiply_reduce_fusion
  27.5 0.7 exponential_convert_fusion
  28.2 0.2 copy-done.2
  28.4 0.4 fusion
  28.9 22.1 %all_to_all.50 = bf16[16,32,128]{2,1,0:T(8,128)(2,1)S(1)} all-to-all(bf16[16,32,128]{2,1,0:T(8,128)(2,1)S(1)} %bitcast.124), channel_id=1, replica_groups=mesh['rows'=16,'centres'=32] {'rows'}, dimensions={0} | all-to-all | bytes 262144 | tf_op jit(solution)/shard_map/all_to_all | solution.py:10
  51.1 11.6 %all_to_all.51 = bf16[16,32,128]{2,1,0:T(8,128)(2,1)S(1)} all-to-all(bf16[16,32,128]{2,1,0:T(8,128)(2,1)S(1)} %broadcast_in_dim.25), channel_id=1, replica_groups=mesh['rows'=16,'centres'=32] {'rows'}, dimensions={0} | all-to-all | bytes 262144 | tf_op jit(solution)/shard_map/all_to_all | solution.py:10
  62.6 0.1 copy.37
  62.7 0.4 fusion.5
  63.2 0.5 fusion.31
  63.8 16.7 %all_to_all.52 = bf16[32,40,128]{2,1,0:T(8,128)(2,1)S(1)} all-to-all(bf16[32,40,128]{2,1,0:T(8,128)(2,1)S(1)} %pad_maximum_fusion), channel_id=1, replica_groups=mesh['rows'=16,'centres'=32] {'centres'}, dimensions={0} | all-to-all | bytes 655360 | tf_op jit(solution)/shard_map/all_to_all | solution.py:10
  80.6 0.7 broadcast_in_dim.28
  81.3 6.8 %all-to-all-start.4 = ((bf16[32,32,128]{2,1,0:T(8,128)(2,1)}), bf16[32,32,128]{2,1,0:T(8,128)(2,1)S(1)}, u32[]{:S(2)}, u32[]{:S(2)}) async-start(bf16[32,32,128]{2,1,0:T(8,128)(2,1)} %broadcast_in_dim.28), calls=%async_computation.4 | async-start | bytes 524288 | tf_op jit(solution)/shard_map/all_to_all | solution.py:10
  88.2 9.6 %all-to-all-done.4 = bf16[32,32,128]{2,1,0:T(8,128)(2,1)S(1)} async-done(((bf16[32,32,128]{2,1,0:T(8,128)(2,1)}), bf16[32,32,128]{2,1,0:T(8,128)(2,1)S(1)}, u32[]{:S(2)}, u32[]{:S(2)}) %all-to-all-start.4) | async-done | bytes 262176 | tf_op jit(solution)/shard_map/all_to_all | solution.py:10
  97.8 0.2 multiply_reduce_fusion.2
  97.9 0.4 fusion.1
  98.5 0.7 pad_maximum_fusion.2
  99.1 7.0 %all-to-all-start.5 = ((bf16[16,40,128]{2,1,0:T(8,128)(2,1)}), bf16[16,40,128]{2,1,0:T(8,128)(2,1)S(1)}, u32[]{:S(2)}, u32[]{:S(2)}) async-start(bf16[16,40,128]{2,1,0:T(8,128)(2,1)} %pad_maximum_fusion.2), calls=%async_computation.5 | async-start | bytes 327680 | tf_op jit(solution)/shard_map/all_to_all | solution.py:10
  106.3 9.5 %all-to-all-done.5 = bf16[16,40,128]{2,1,0:T(8,128)(2,1)S(1)} async-done(((bf16[16,40,128]{2,1,0:T(8,128)(2,1)}), bf16[16,40,128]{2,1,0:T(8,128)(2,1)S(1)}, u32[]{:S(2)}, u32[]{:S(2)}) %all-to-all-start.5) | async-done | bytes 163872 | tf_op jit(solution)/shard_map/all_to_all | solution.py:10
  115.9 11.6 %all_to_all.53 = bf16[16,32,128]{2,1,0:T(8,128)(2,1)S(1)} all-to-all(bf16[16,32,128]{2,1,0:T(8,128)(2,1)S(1)} %broadcast_in_dim.31), channel_id=1, replica_groups=mesh['rows'=16,'centres'=32] {'rows'}, dimensions={0} | all-to-all | bytes 262144 | tf_op jit(solution)/shard_map/all_to_all | solution.py:10
  127.6 0.4 fusion.7
  128.1 0.5 convolution_convert_fusion
  128.6 15.4 %all_to_all.54 = bf16[32,40,128]{2,1,0:T(8,128)(2,1)S(1)} all-to-all(bf16[32,40,128]{2,1,0:T(8,128)(2,1)S(1)} %pad_maximum_fusion.1), channel_id=1, replica_groups=mesh['rows'=16,'centres'=32] {'centres'}, dimensions={0} | all-to-all | bytes 655360 | tf_op jit(solution)/shard_map/all_to_all | solution.py:10
  144.2 16.2 %all_to_all.55 = bf16[32,32,128]{2,1,0:T(8,128)(2,1)S(1)} all-to-all(bf16[32,32,128]{2,1,0:T(8,128)(2,1)S(1)} %broadcast_in_dim.68), channel_id=1, replica_groups=mesh['rows'=16,'centres'=32] {'centres'}, dimensions={0} | all-to-all | bytes 524288 | tf_op jit(solution)/shard_map/all_to_all | solution.py:10
  160.4 0.2 multiply_reduce_fusion.1
  160.6 13.2 %all_to_all.56 = f32[16,1,128]{2,1,0:T(1,128)S(1)} all-to-all(f32[16,1,128]{2,1,0:T(1,128)S(1)} %broadcast_in_dim.69), channel_id=1, replica_groups=mesh['rows'=16,'centres'=32] {'rows'}, dimensions={0} | all-to-all | bytes 16384 | tf_op jit(solution)/shard_map/all_to_all | solution.py:10
  173.8 0.1 fusion.6
  173.9 0.8 copy.41
  174.8 0.9 fusion.2
  (48 shorter events, 1.0 us)
Async XLA Ops:
  0.6 62.1 %copy-start = (bf16[512,512]{1,0:T(8,128)(2,1)S(1)}, bf16[512,512]{1,0:T(8,128)(2,1)}, u32[]{:S(2)}) copy-start(bf16[512,512]{1,0:T(8,128)(2,1)} %param.7) | copy-start | bytes 1572868
  0.6 12.1 %copy-start.1 = (bf16[512,256]{1,0:T(8,128)(2,1)S(1)}, bf16[512,256]{1,0:T(8,128)(2,1)}, u32[]{:S(2)}) copy-start(bf16[512,256]{1,0:T(8,128)(2,1)} %param.6) | copy-start | bytes 786436
  2.3 25.0 %all-to-all-start = ((bf16[32,8,1024]{2,1,0:T(8,128)(2,1)}), bf16[32,8,1024]{2,1,0:T(8,128)(2,1)S(1)}, u32[]{:S(2)}, u32[]{:S(2)}) async-start(bf16[32,8,1024]{2,1,0:T(8,128)(2,1)} %broadcast_in_dim.24), calls=%async_computation | async-start | bytes 1048576 | tf_op jit(solution)/shard_map/all_to_all | solution.py:10
  27.5 1.0 copy-start.2
  81.3 16.5 %all-to-all-start.4 = ((bf16[32,32,128]{2,1,0:T(8,128)(2,1)}), bf16[32,32,128]{2,1,0:T(8,128)(2,1)S(1)}, u32[]{:S(2)}, u32[]{:S(2)}) async-start(bf16[32,32,128]{2,1,0:T(8,128)(2,1)} %broadcast_in_dim.28), calls=%async_computation.4 | async-start | bytes 524288 | tf_op jit(solution)/shard_map/all_to_all | solution.py:10
  99.1 16.6 %all-to-all-start.5 = ((bf16[16,40,128]{2,1,0:T(8,128)(2,1)}), bf16[16,40,128]{2,1,0:T(8,128)(2,1)S(1)}, u32[]{:S(2)}, u32[]{:S(2)}) async-start(bf16[16,40,128]{2,1,0:T(8,128)(2,1)} %pad_maximum_fusion.2), calls=%async_computation.5 | async-start | bytes 327680 | tf_op jit(solution)/shard_map/all_to_all | solution.py:10

commit v2 on v1

v2 whole, which is shorter than its diff:
```python
import jax
import jax.numpy as jnp
from jax import lax
from jax.sharding import Mesh, PartitionSpec as P

RIDGE_WEIGHT = 0.02


def exchanged(tiles, axis):
    return lax.all_to_all(tiles, axis, split_axis=0, concat_axis=0, tiled=True)


def copies_of(value, axis):
    copies = jnp.broadcast_to(value, (lax.axis_size(axis), *value.shape))
    return exchanged(copies, axis)


def two_halves(rows):
    high = rows.astype(jnp.bfloat16)
    low = (rows - high.astype(jnp.float32)).astype(jnp.bfloat16)
    return high, low


def extra_rows(sums):
    parts = [p[None, :] for s in sums for p in two_halves(s)]
    return jnp.concatenate((parts * 4)[:8], axis=0)


def with_sums(tiles, sums):
    if not sums:
        return tiles
    rows = extra_rows(sums)
    return jnp.concatenate(
        [tiles, jnp.broadcast_to(rows, (tiles.shape[0], *rows.shape))], axis=1
    )


def totalled(arrived, share, count):
    total = arrived.astype(jnp.float32).sum(axis=0)
    sums = [total[share + 2 * i] + total[share + 2 * i + 1] for i in range(count)]
    return total[:share], sums


def summed_shares(partial, sums, axis):
    size = lax.axis_size(axis)
    share = partial.shape[0] // size
    tiles = partial.astype(jnp.bfloat16).reshape(size, share, partial.shape[1])
    return totalled(exchanged(with_sums(tiles, sums), axis), share, len(sums))


def summed_directly(share, sums, axis):
    tiles = jnp.broadcast_to(share.astype(jnp.bfloat16), (lax.axis_size(axis), *share.shape))
    return totalled(exchanged(with_sums(tiles, sums), axis), share.shape[0], len(sums))


def summed_in_plane(partial, sums):
    share, sums = summed_shares(partial, sums, "y")
    return summed_directly(share, sums, "x")


def per_device(features, targets, centre_points, precond):
    group_rows = float(features.shape[0])
    gathered = copies_of(features.T, ("x", "y")).reshape(-1, features.shape[0])
    gathered, centre_points = lax.optimization_barrier((gathered, centre_points))
    feature_count = gathered.shape[0]
    gathered_float = gathered.astype(jnp.float32)
    centre_float = centre_points.astype(jnp.float32)
    row_scale = 1.0 / jnp.sqrt(jnp.mean(gathered_float * gathered_float, axis=0) + 1e-06)
    centre_scale = 1.0 / jnp.sqrt(jnp.mean(centre_float * centre_float, axis=1) + 1e-06)
    inner_products = jnp.dot(centre_points, gathered, preferred_element_type=jnp.float32)
    cosine = (
        inner_products * row_scale[None, :] * centre_scale[:, None] / jnp.float32(feature_count)
    )
    kernel = jnp.exp(8.0 * (cosine - 1.0)).astype(jnp.bfloat16)

    def transposed(values):
        return jnp.dot(kernel, values, preferred_element_type=jnp.float32)

    def forward(values):
        return jnp.einsum(
            "cr,ct->rt", kernel, values.astype(jnp.bfloat16), preferred_element_type=jnp.float32
        )

    def precondition(residual):
        return jnp.dot(precond, residual, preferred_element_type=jnp.float32)

    def whole(share, axis):
        return copies_of(share.astype(jnp.bfloat16), axis).reshape(-1, share.shape[1])

    def column_sum(a, b):
        return jnp.sum(a * b, axis=0)

    residual_share, _ = summed_shares(
        transposed(targets) / jnp.sqrt(jnp.float32(group_rows)), [], "rows"
    )
    residual = whole(residual_share, "rows")
    direction = precondition(residual)
    sums = [
        column_sum(residual.astype(jnp.float32), direction),
        column_sum(direction, direction),
    ]
    rows_share, (product_now, direction_sq) = summed_in_plane(forward(direction), sums)
    rounded = whole(rows_share, "y")
    rounded_float = rounded.astype(jnp.float32)
    ridge_part = (RIDGE_WEIGHT / lax.axis_size("rows")) * direction
    applied_share, (rows_sq,) = summed_shares(
        transposed(rounded) / group_rows + ridge_part, [column_sum(rounded_float, rounded_float)], "rows"
    )
    step_size = product_now / (rows_sq / group_rows + RIDGE_WEIGHT * direction_sq)
    residual_share = residual_share - step_size * applied_share
    residual = whole(residual_share, "rows")
    scaled = precondition(residual)
    sums = [
        column_sum(residual.astype(jnp.float32), scaled),
        column_sum(scaled, scaled),
        column_sum(scaled, direction),
    ]
    scaled_rows_share, (product_next, scaled_sq, cross_term) = summed_in_plane(
        forward(scaled), sums
    )
    momentum = product_next / product_now
    next_sq = scaled_sq + 2.0 * momentum * cross_term + momentum * momentum * direction_sq
    next_direction = scaled + momentum * direction
    next_rows_share = scaled_rows_share + momentum * rows_share
    next_rows = whole(next_rows_share, "y").astype(jnp.float32)
    rows_sq = jnp.sum(copies_of(column_sum(next_rows, next_rows)[None], "rows"), axis=(0, 1))
    next_step = product_next / (rows_sq / group_rows + RIDGE_WEIGHT * next_sq)
    coefficients = step_size * direction + next_step * next_direction
    fitted = step_size * rounded_float + next_step * next_rows
    return (coefficients, fitted)


def solution(mesh):
    rows, centres = mesh.devices.shape
    split = Mesh(mesh.devices.reshape(rows, centres // 8, 8), ("rows", "x", "y"))
    plane = ("x", "y")
    return jax.shard_map(
        per_device,
        mesh=split,
        in_specs=(P("rows", plane), P("rows", None), P(plane, None), P(plane, None)),
        out_specs=(P(plane, None), P("rows", None)),
        check_vma=False,
    )
```

time: 176 us -> 178 us (1.011)
  blocking collectives: 107 us -> 168 us
  waiting for transfers between devices: 33.4 us -> 0 us
  starting transfers between devices: 24.3 us -> 0 us
    all_to_all x7 -> x12, blocking collectives: 107 us -> 168 us  [exchanged(): return lax.all_to_all(tiles, axis, split_axis=0, concat_axis=0, tiled=True)]
    all_to_all x3 -> x0, waiting for transfers between devices: 33.4 us -> none  [exchanged(): return lax.all_to_all(tiles, axis, split_axis=0, concat_axis=0, tiled=True)]
    all_to_all x3 -> x0, starting transfers between devices: 24.3 us -> none  [exchanged(): return lax.all_to_all(tiles, axis, split_axis=0, concat_axis=0, tiled=True)]
  transfers between devices with their start and end apart: 3 -> 0, of which waited for: 3 -> 0; matrix products, arithmetic and copies ran while one was open for 0% -> 0% of each run, Pallas kernels for 0% -> 0%
where the time goes in v2:
time: 178 us; the launch traced here: 177 us
  blocking collectives  168 us (94%)
  matrix products  3.42 us (2%)
  local copies, waits for them, and re-layouts  2.67 us (2%)
  other arithmetic  2.02 us (1%)
    all_to_all x12, blocking collectives, exchanged(): return lax.all_to_all(tiles, axis, split_axis=0, concat_axis=0, tiled=True)  168 us

profile of v2, /device:TPU:1, one launch (start us, length us, event | category | flops | bytes accessed | tf_op | source)
XLA Modules:
  0.0 177.3 jit_solution(15829284051366987386)
XLA Ops:
  0.6 0.0 copy-start
  0.7 0.8 broadcast_in_dim.26
  1.5 24.8 %all_to_all.60 = bf16[32,8,1024]{2,1,0:T(8,128)(2,1)S(1)} all-to-all(bf16[32,8,1024]{2,1,0:T(8,128)(2,1)S(1)} %broadcast_in_dim.26), channel_id=1, replica_groups=mesh['rows'=16,'x'=4,'y'=8] {'x','y'}, dimensions={0} | all-to-all | bytes 1048576 | tf_op jit(solution)/shard_map/all_to_all | solution.py:10
  26.3 0.1 multiply_reduce_fusion.3
  26.5 0.1 multiply_reduce_fusion
  26.6 0.7 exponential_convert_fusion
  27.3 0.2 copy-done.2
  27.6 0.4 fusion.1
  28.0 22.1 %all_to_all.61 = bf16[16,32,128]{2,1,0:T(8,128)(2,1)S(1)} all-to-all(bf16[16,32,128]{2,1,0:T(8,128)(2,1)S(1)} %bitcast.94), channel_id=1, replica_groups=mesh['rows'=16,'x'=4,'y'=8] {'rows'}, dimensions={0} | all-to-all | bytes 262144 | tf_op jit(solution)/shard_map/all_to_all | solution.py:10
  50.2 11.6 %all_to_all.62 = bf16[16,32,128]{2,1,0:T(8,128)(2,1)S(1)} all-to-all(bf16[16,32,128]{2,1,0:T(8,128)(2,1)S(1)} %broadcast_in_dim.27), channel_id=1, replica_groups=mesh['rows'=16,'x'=4,'y'=8] {'rows'}, dimensions={0} | all-to-all | bytes 262144 | tf_op jit(solution)/shard_map/all_to_all | solution.py:10
  61.8 0.1 copy.21
  61.9 0.4 multiply_reduce_fusion.7
  62.3 0.5 convolution_convert_fusion.1
  62.9 16.7 %all_to_all.63 = bf16[8,136,128]{2,1,0:T(8,128)(2,1)S(1)} all-to-all(bf16[8,136,128]{2,1,0:T(8,128)(2,1)S(1)} %pad_maximum_fusion), channel_id=1, replica_groups=mesh['rows'=16,'x'=4,'y'=8] {'y'}, dimensions={0} | all-to-all | bytes 557056 | tf_op jit(solution)/shard_map/all_to_all | solution.py:10
  79.8 7.3 %all_to_all.64 = bf16[4,136,128]{2,1,0:T(8,128)(2,1)S(1)} all-to-all(bf16[4,136,128]{2,1,0:T(8,128)(2,1)S(1)} %pad_maximum_fusion.3), channel_id=1, replica_groups=mesh['rows'=16,'x'=4,'y'=8] {'x'}, dimensions={0} | all-to-all | bytes 278528 | tf_op jit(solution)/shard_map/all_to_all | solution.py:10
  87.1 12.1 %all_to_all.65 = bf16[8,128,128]{2,1,0:T(8,128)(2,1)S(1)} all-to-all(bf16[8,128,128]{2,1,0:T(8,128)(2,1)S(1)} %broadcast_in_dim.31), channel_id=1, replica_groups=mesh['rows'=16,'x'=4,'y'=8] {'y'}, dimensions={0} | all-to-all | bytes 524288 | tf_op jit(solution)/shard_map/all_to_all | solution.py:10
  99.2 0.2 multiply_reduce_fusion.2
  99.4 0.5 fusion.2
  99.9 0.1 copy.23
  100.1 15.1 %all_to_all.66 = bf16[16,40,128]{2,1,0:T(8,128)(2,1)S(1)} all-to-all(bf16[16,40,128]{2,1,0:T(8,128)(2,1)S(1)} %pad_maximum_fusion.2), channel_id=1, replica_groups=mesh['rows'=16,'x'=4,'y'=8] {'rows'}, dimensions={0} | all-to-all | bytes 327680 | tf_op jit(solution)/shard_map/all_to_all | solution.py:10
  115.3 11.6 %all_to_all.67 = bf16[16,32,128]{2,1,0:T(8,128)(2,1)S(1)} all-to-all(bf16[16,32,128]{2,1,0:T(8,128)(2,1)S(1)} %broadcast_in_dim.33), channel_id=1, replica_groups=mesh['rows'=16,'x'=4,'y'=8] {'rows'}, dimensions={0} | all-to-all | bytes 262144 | tf_op jit(solution)/shard_map/all_to_all | solution.py:10
  126.9 0.1 copy.24
  127.0 0.4 multiply_reduce_fusion.4
  127.5 0.5 convolution_convert_fusion
  128.0 15.0 %all_to_all.68 = bf16[8,136,128]{2,1,0:T(8,128)(2,1)S(1)} all-to-all(bf16[8,136,128]{2,1,0:T(8,128)(2,1)S(1)} %pad_maximum_fusion.1), channel_id=1, replica_groups=mesh['rows'=16,'x'=4,'y'=8] {'y'}, dimensions={0} | all-to-all | bytes 557056 | tf_op jit(solution)/shard_map/all_to_all | solution.py:10
  143.2 7.3 %all_to_all.69 = bf16[4,136,128]{2,1,0:T(8,128)(2,1)S(1)} all-to-all(bf16[4,136,128]{2,1,0:T(8,128)(2,1)S(1)} %pad_maximum_fusion.4), channel_id=1, replica_groups=mesh['rows'=16,'x'=4,'y'=8] {'x'}, dimensions={0} | all-to-all | bytes 278528 | tf_op jit(solution)/shard_map/all_to_all | solution.py:10
  150.6 11.7 %all_to_all.70 = bf16[8,128,128]{2,1,0:T(8,128)(2,1)S(1)} all-to-all(bf16[8,128,128]{2,1,0:T(8,128)(2,1)S(1)} %broadcast_in_dim.37), channel_id=1, replica_groups=mesh['rows'=16,'x'=4,'y'=8] {'y'}, dimensions={0} | all-to-all | bytes 524288 | tf_op jit(solution)/shard_map/all_to_all | solution.py:10
  162.3 0.2 multiply_reduce_fusion.1
  162.5 13.0 %all_to_all.71 = f32[16,1,128]{2,1,0:T(1,128)S(1)} all-to-all(f32[16,1,128]{2,1,0:T(1,128)S(1)} %broadcast_in_dim.38), channel_id=1, replica_groups=mesh['rows'=16,'x'=4,'y'=8] {'rows'}, dimensions={0} | all-to-all | bytes 16384 | tf_op jit(solution)/shard_map/all_to_all | solution.py:10
  175.5 0.1 multiply_add_fusion
  175.6 0.8 copy.26
  176.4 0.9 fusion.3
  (56 shorter events, 0.8 us)
Async XLA Ops:
  0.6 61.3 %copy-start = (bf16[512,512]{1,0:T(8,128)(2,1)S(1)}, bf16[512,512]{1,0:T(8,128)(2,1)}, u32[]{:S(2)}) copy-start(bf16[512,512]{1,0:T(8,128)(2,1)} %param.7) | copy-start | bytes 1572868
  0.6 25.7 %copy-start.1 = (bf16[512,256]{1,0:T(8,128)(2,1)S(1)}, bf16[512,256]{1,0:T(8,128)(2,1)}, u32[]{:S(2)}) copy-start(bf16[512,256]{1,0:T(8,128)(2,1)} %param.6) | copy-start | bytes 786436
  26.6 1.0 copy-start.2

commit v3 on v2

--- a/solution.py
+++ b/solution.py
@@ -54,13 +54,13 @@
 
 
 def summed_in_plane(partial, sums):
-    share, sums = summed_shares(partial, sums, "y")
-    return summed_directly(share, sums, "x")
+    return summed_shares(partial, sums, ("x", "y"))
 
 
 def per_device(features, targets, centre_points, precond):
     group_rows = float(features.shape[0])
-    gathered = copies_of(features.T, ("x", "y")).reshape(-1, features.shape[0])
+    group_parts = copies_of(features.T, "y")
+    gathered = copies_of(group_parts, "x").reshape(-1, features.shape[0])
     gathered, centre_points = lax.optimization_barrier((gathered, centre_points))
     feature_count = gathered.shape[0]
     gathered_float = gathered.astype(jnp.float32)
@@ -100,7 +100,7 @@
         column_sum(direction, direction),
     ]
     rows_share, (product_now, direction_sq) = summed_in_plane(forward(direction), sums)
-    rounded = whole(rows_share, "y")
+    rounded = whole(rows_share, ("x", "y"))
     rounded_float = rounded.astype(jnp.float32)
     ridge_part = (RIDGE_WEIGHT / lax.axis_size("rows")) * direction
     applied_share, (rows_sq,) = summed_shares(
@@ -122,7 +122,7 @@
     next_sq = scaled_sq + 2.0 * momentum * cross_term + momentum * momentum * direction_sq
     next_direction = scaled + momentum * direction
     next_rows_share = scaled_rows_share + momentum * rows_share
-    next_rows = whole(next_rows_share, "y").astype(jnp.float32)
+    next_rows = whole(next_rows_share, ("x", "y")).astype(jnp.float32)
     rows_sq = jnp.sum(copies_of(column_sum(next_rows, next_rows)[None], "rows"), axis=(0, 1))
     next_step = product_next / (rows_sq / group_rows + RIDGE_WEIGHT * next_sq)
     coefficients = step_size * direction + next_step * next_direction

time: 178 us -> 172 us (0.966)
  blocking collectives: 168 us -> 163 us
    all_to_all x12 -> x11, blocking collectives: 168 us -> 163 us  [exchanged(): return lax.all_to_all(tiles, axis, split_axis=0, concat_axis=0, tiled=True)]
where the time goes in v3:
time: 172 us
  blocking collectives  163 us (95%)
  matrix products  3.42 us (2%)
  local copies, waits for them, and re-layouts  2.56 us (1%)
  other arithmetic  1.97 us (1%)
    all_to_all x11, blocking collectives, exchanged(): return lax.all_to_all(tiles, axis, split_axis=0, concat_axis=0, tiled=True)  163 us

profile of v3, /device:TPU:1, one launch (start us, length us, event | category | flops | bytes accessed | tf_op | source)
XLA Modules:
  0.0 171.9 jit_solution(5895795375022698209)
XLA Ops:
  0.7 0.8 broadcast_in_dim.20
  1.5 15.4 %all_to_all.55 = bf16[8,8,1024]{2,1,0:T(8,128)(2,1)S(1)} all-to-all(bf16[8,8,1024]{2,1,0:T(8,128)(2,1)S(1)} %broadcast_in_dim.20), channel_id=1, replica_groups=mesh['rows'=16,'x'=4,'y'=8] {'y'}, dimensions={0} | all-to-all | bytes 262144 | tf_op jit(solution)/shard_map/all_to_all | solution.py:10
  16.9 10.6 %all_to_all.56 = bf16[4,8,8,1024]{3,2,1,0:T(8,128)(2,1)S(1)} all-to-all(bf16[4,8,8,1024]{3,2,1,0:T(8,128)(2,1)S(1)} %broadcast_in_dim.21), channel_id=1, replica_groups=mesh['rows'=16,'x'=4,'y'=8] {'x'}, dimensions={0} | all-to-all | bytes 1048576 | tf_op jit(solution)/shard_map/all_to_all | solution.py:10
  27.5 0.1 multiply_reduce_fusion.3
  27.6 0.1 multiply_reduce_fusion
  27.8 0.7 exponential_convert_fusion
  28.5 0.2 copy-done.2
  28.7 0.4 fusion.1
  29.2 22.7 %all_to_all.57 = bf16[16,32,128]{2,1,0:T(8,128)(2,1)S(1)} all-to-all(bf16[16,32,128]{2,1,0:T(8,128)(2,1)S(1)} %bitcast.94), channel_id=1, replica_groups=mesh['rows'=16,'x'=4,'y'=8] {'rows'}, dimensions={0} | all-to-all | bytes 262144 | tf_op jit(solution)/shard_map/all_to_all | solution.py:10
  52.0 11.6 %all_to_all.58 = bf16[16,32,128]{2,1,0:T(8,128)(2,1)S(1)} all-to-all(bf16[16,32,128]{2,1,0:T(8,128)(2,1)S(1)} %broadcast_in_dim.22), channel_id=1, replica_groups=mesh['rows'=16,'x'=4,'y'=8] {'rows'}, dimensions={0} | all-to-all | bytes 262144 | tf_op jit(solution)/shard_map/all_to_all | solution.py:10
  63.5 0.1 copy.21
  63.6 0.4 multiply_reduce_fusion.7
  64.1 0.5 convolution_convert_fusion.1
  64.6 14.9 %all_to_all.59 = bf16[32,40,128]{2,1,0:T(8,128)(2,1)S(1)} all-to-all(bf16[32,40,128]{2,1,0:T(8,128)(2,1)S(1)} %pad_maximum_fusion), channel_id=1, replica_groups=mesh['rows'=16,'x'=4,'y'=8] {'x','y'}, dimensions={0} | all-to-all | bytes 655360 | tf_op jit(solution)/shard_map/all_to_all | solution.py:10
  79.5 0.1 convert_reduce_fusion.1
  79.6 15.8 %all_to_all.60 = bf16[32,32,128]{2,1,0:T(8,128)(2,1)S(1)} all-to-all(bf16[32,32,128]{2,1,0:T(8,128)(2,1)S(1)} %broadcast_in_dim.24), channel_id=1, replica_groups=mesh['rows'=16,'x'=4,'y'=8] {'x','y'}, dimensions={0} | all-to-all | bytes 524288 | tf_op jit(solution)/shard_map/all_to_all | solution.py:10
  95.5 0.2 multiply_reduce_fusion.2
  95.6 0.5 fusion.2
  96.1 0.1 copy.23
  96.3 15.7 %all_to_all.61 = bf16[16,40,128]{2,1,0:T(8,128)(2,1)S(1)} all-to-all(bf16[16,40,128]{2,1,0:T(8,128)(2,1)S(1)} %pad_maximum_fusion.2), channel_id=1, replica_groups=mesh['rows'=16,'x'=4,'y'=8] {'rows'}, dimensions={0} | all-to-all | bytes 327680 | tf_op jit(solution)/shard_map/all_to_all | solution.py:10
  112.1 11.6 %all_to_all.62 = bf16[16,32,128]{2,1,0:T(8,128)(2,1)S(1)} all-to-all(bf16[16,32,128]{2,1,0:T(8,128)(2,1)S(1)} %broadcast_in_dim.26), channel_id=1, replica_groups=mesh['rows'=16,'x'=4,'y'=8] {'rows'}, dimensions={0} | all-to-all | bytes 262144 | tf_op jit(solution)/shard_map/all_to_all | solution.py:10
  123.7 0.1 copy.24
  123.8 0.4 multiply_reduce_fusion.4
  124.3 0.5 convolution_convert_fusion
  124.9 15.4 %all_to_all.63 = bf16[32,40,128]{2,1,0:T(8,128)(2,1)S(1)} all-to-all(bf16[32,40,128]{2,1,0:T(8,128)(2,1)S(1)} %pad_maximum_fusion.1), channel_id=1, replica_groups=mesh['rows'=16,'x'=4,'y'=8] {'x','y'}, dimensions={0} | all-to-all | bytes 655360 | tf_op jit(solution)/shard_map/all_to_all | solution.py:10
  140.3 0.1 convert_reduce_fusion
  140.4 16.3 %all_to_all.64 = bf16[32,32,128]{2,1,0:T(8,128)(2,1)S(1)} all-to-all(bf16[32,32,128]{2,1,0:T(8,128)(2,1)S(1)} %broadcast_in_dim.28), channel_id=1, replica_groups=mesh['rows'=16,'x'=4,'y'=8] {'x','y'}, dimensions={0} | all-to-all | bytes 524288 | tf_op jit(solution)/shard_map/all_to_all | solution.py:10
  156.7 0.2 multiply_reduce_fusion.1
  156.8 13.2 %all_to_all.65 = f32[16,1,128]{2,1,0:T(1,128)S(1)} all-to-all(f32[16,1,128]{2,1,0:T(1,128)S(1)} %broadcast_in_dim.29), channel_id=1, replica_groups=mesh['rows'=16,'x'=4,'y'=8] {'rows'}, dimensions={0} | all-to-all | bytes 16384 | tf_op jit(solution)/shard_map/all_to_all | solution.py:10
  170.0 0.1 multiply_add_fusion
  170.2 0.8 copy.26
  171.0 0.9 fusion.3
  (42 shorter events, 0.6 us)
Async XLA Ops:
  0.6 63.0 %copy-start = (bf16[512,512]{1,0:T(8,128)(2,1)S(1)}, bf16[512,512]{1,0:T(8,128)(2,1)}, u32[]{:S(2)}) copy-start(bf16[512,512]{1,0:T(8,128)(2,1)} %param.7) | copy-start | bytes 1572868
  0.6 26.8 %copy-start.1 = (bf16[512,256]{1,0:T(8,128)(2,1)S(1)}, bf16[512,256]{1,0:T(8,128)(2,1)}, u32[]{:S(2)}) copy-start(bf16[512,256]{1,0:T(8,128)(2,1)} %param.6) | copy-start | bytes 786436
  27.8 1.0 copy-start.2

commit v4 on v3

--- a/solution.py
+++ b/solution.py
@@ -1,6 +1,7 @@
 import jax
 import jax.numpy as jnp
 from jax import lax
+from jax.experimental.layout import Layout, with_layout_constraint
 from jax.sharding import Mesh, PartitionSpec as P
 
 RIDGE_WEIGHT = 0.02
@@ -15,42 +16,20 @@
     return exchanged(copies, axis)
 
 
-def two_halves(rows):
-    high = rows.astype(jnp.bfloat16)
-    low = (rows - high.astype(jnp.float32)).astype(jnp.bfloat16)
-    return high, low
-
-
-def extra_rows(sums):
-    parts = [p[None, :] for s in sums for p in two_halves(s)]
-    return jnp.concatenate((parts * 4)[:8], axis=0)
-
-
-def with_sums(tiles, sums):
-    if not sums:
-        return tiles
-    rows = extra_rows(sums)
-    return jnp.concatenate(
-        [tiles, jnp.broadcast_to(rows, (tiles.shape[0], *rows.shape))], axis=1
-    )
-
-
-def totalled(arrived, share, count):
-    total = arrived.astype(jnp.float32).sum(axis=0)
-    sums = [total[share + 2 * i] + total[share + 2 * i + 1] for i in range(count)]
-    return total[:share], sums
-
-
 def summed_shares(partial, sums, axis):
     size = lax.axis_size(axis)
-    share = partial.shape[0] // size
-    tiles = partial.astype(jnp.bfloat16).reshape(size, share, partial.shape[1])
-    return totalled(exchanged(with_sums(tiles, sums), axis), share, len(sums))
-
-
-def summed_directly(share, sums, axis):
-    tiles = jnp.broadcast_to(share.astype(jnp.bfloat16), (lax.axis_size(axis), *share.shape))
-    return totalled(exchanged(with_sums(tiles, sums), axis), share.shape[0], len(sums))
+    width = partial.shape[1]
+    if not sums:
+        tiles = partial.astype(jnp.bfloat16).reshape(size, -1, width)
+        return exchanged(tiles, axis).astype(jnp.float32).sum(axis=0), []
+    pairs = partial.shape[0] // size // 2
+    tiles = partial.astype(jnp.bfloat16).reshape(size, pairs, 2, width)
+    rows = list(sums) + [sums[0]] * (len(sums) % 2)
+    rows = jnp.stack(rows).astype(jnp.bfloat16).reshape(1, -1, 2, width)
+    tiles = jnp.concatenate([tiles, jnp.broadcast_to(rows, (size, *rows.shape[1:]))], axis=1)
+    total = exchanged(tiles, axis).astype(jnp.float32).sum(axis=0)
+    totals = [total[pairs + i // 2, i % 2] for i in range(len(sums))]
+    return total[:pairs].reshape(-1, width), totals
 
 
 def summed_in_plane(partial, sums):
@@ -82,7 +61,8 @@
         )
 
     def precondition(residual):
-        return jnp.dot(precond, residual, preferred_element_type=jnp.float32)
+        product = jnp.dot(precond, residual, preferred_element_type=jnp.float32)
+        return with_layout_constraint(product, Layout((0, 1)))
 
     def whole(share, axis):
         return copies_of(share.astype(jnp.bfloat16), axis).reshape(-1, share.shape[1])

time: 172 us -> 171 us (level)
  blocking collectives: 163 us -> 161 us
  other arithmetic: 1.97 us -> 3.93 us
    all_to_all x11, blocking collectives: 163 us -> 161 us  [exchanged(): return lax.all_to_all(tiles, axis, split_axis=0, concat_axis=0, tiled=True)]
where the time goes in v4:
time: 171 us; the launch traced here: 170 us
  blocking collectives  161 us (94%)
  other arithmetic  3.93 us (2%)
  matrix products  3.16 us (2%)
    all_to_all x11, blocking collectives, exchanged(): return lax.all_to_all(tiles, axis, split_axis=0, concat_axis=0, tiled=True)  161 us

profile of v4, /device:TPU:1, one launch (start us, length us, event | category | flops | bytes accessed | tf_op | source)
XLA Modules:
  0.0 170.1 jit_solution(16019976925763960189)
XLA Ops:
  0.7 0.8 broadcast_in_dim.20
  1.5 15.4 %all_to_all.55 = bf16[8,8,1024]{2,1,0:T(8,128)(2,1)S(1)} all-to-all(bf16[8,8,1024]{2,1,0:T(8,128)(2,1)S(1)} %broadcast_in_dim.20), channel_id=1, replica_groups=mesh['rows'=16,'x'=4,'y'=8] {'y'}, dimensions={0} | all-to-all | bytes 262144 | tf_op jit(solution)/shard_map/all_to_all | solution.py:11
  16.9 10.6 %all_to_all.56 = bf16[4,8,8,1024]{3,2,1,0:T(8,128)(2,1)S(1)} all-to-all(bf16[4,8,8,1024]{3,2,1,0:T(8,128)(2,1)S(1)} %broadcast_in_dim.21), channel_id=1, replica_groups=mesh['rows'=16,'x'=4,'y'=8] {'x'}, dimensions={0} | all-to-all | bytes 1048576 | tf_op jit(solution)/shard_map/all_to_all | solution.py:11
  27.5 0.1 multiply_reduce_fusion.3
  27.6 0.1 multiply_reduce_fusion
  27.8 0.7 exponential_convert_fusion
  28.5 0.2 copy-done.2
  28.7 0.4 fusion.1
  29.2 22.7 %all_to_all.57 = bf16[16,32,128]{2,1,0:T(8,128)(2,1)S(1)} all-to-all(bf16[16,32,128]{2,1,0:T(8,128)(2,1)S(1)} %bitcast.103), channel_id=1, replica_groups=mesh['rows'=16,'x'=4,'y'=8] {'rows'}, dimensions={0} | all-to-all | bytes 262144 | tf_op jit(solution)/shard_map/all_to_all | solution.py:11
  52.0 11.6 %all_to_all.58 = bf16[16,32,128]{2,1,0:T(8,128)(2,1)S(1)} all-to-all(bf16[16,32,128]{2,1,0:T(8,128)(2,1)S(1)} %broadcast_in_dim.22), channel_id=1, replica_groups=mesh['rows'=16,'x'=4,'y'=8] {'rows'}, dimensions={0} | all-to-all | bytes 262144 | tf_op jit(solution)/shard_map/all_to_all | solution.py:11
  63.5 0.3 multiply_reduce_fusion.8
  63.8 0.5 convolution_convert_fusion.1
  64.4 0.4 pad_maximum_fusion.1
  64.7 13.8 %all_to_all.59 = bf16[32,17,2,128]{3,2,1,0:T(2,128)(2,1)S(1)} all-to-all(bf16[32,17,2,128]{3,2,1,0:T(2,128)(2,1)S(1)} %pad_maximum_fusion.1), channel_id=1, replica_groups=mesh['rows'=16,'x'=4,'y'=8] {'x','y'}, dimensions={0} | all-to-all | bytes 557056 | tf_op jit(solution)/shard_map/all_to_all | solution.py:11
  78.5 0.2 convert_reduce_fusion.1
  78.8 15.9 %all_to_all.60 = bf16[32,32,128]{2,1,0:T(8,128)(2,1)S(1)} all-to-all(bf16[32,32,128]{2,1,0:T(8,128)(2,1)S(1)} %broadcast_in_dim.24), channel_id=1, replica_groups=mesh['rows'=16,'x'=4,'y'=8] {'x','y'}, dimensions={0} | all-to-all | bytes 524288 | tf_op jit(solution)/shard_map/all_to_all | solution.py:11
  94.7 0.2 multiply_reduce_fusion.2
  94.9 0.4 fusion.2
  95.3 0.2 pad_maximum_fusion.2
  95.5 15.5 %all_to_all.61 = bf16[16,17,2,128]{3,2,1,0:T(2,128)(2,1)S(1)} all-to-all(bf16[16,17,2,128]{3,2,1,0:T(2,128)(2,1)S(1)} %pad_maximum_fusion.2), channel_id=1, replica_groups=mesh['rows'=16,'x'=4,'y'=8] {'rows'}, dimensions={0} | all-to-all | bytes 278528 | tf_op jit(solution)/shard_map/all_to_all | solution.py:11
  111.0 0.1 convert_reduce_fusion.2
  111.2 11.3 %all_to_all.62 = bf16[16,32,128]{2,1,0:T(8,128)(2,1)S(1)} all-to-all(bf16[16,32,128]{2,1,0:T(8,128)(2,1)S(1)} %broadcast_in_dim.52), channel_id=1, replica_groups=mesh['rows'=16,'x'=4,'y'=8] {'rows'}, dimensions={0} | all-to-all | bytes 262144 | tf_op jit(solution)/shard_map/all_to_all | solution.py:11
  122.5 0.3 multiply_reduce_fusion.5
  122.8 0.5 convolution_convert_fusion
  123.4 0.4 pad_maximum_fusion
  123.8 14.6 %all_to_all.63 = bf16[32,18,2,128]{3,2,1,0:T(2,128)(2,1)S(1)} all-to-all(bf16[32,18,2,128]{3,2,1,0:T(2,128)(2,1)S(1)} %pad_maximum_fusion), channel_id=1, replica_groups=mesh['rows'=16,'x'=4,'y'=8] {'x','y'}, dimensions={0} | all-to-all | bytes 589824 | tf_op jit(solution)/shard_map/all_to_all | solution.py:11
  138.4 0.2 convert_reduce_fusion
  138.7 16.3 %all_to_all.64 = bf16[32,32,128]{2,1,0:T(8,128)(2,1)S(1)} all-to-all(bf16[32,32,128]{2,1,0:T(8,128)(2,1)S(1)} %broadcast_in_dim.54), channel_id=1, replica_groups=mesh['rows'=16,'x'=4,'y'=8] {'x','y'}, dimensions={0} | all-to-all | bytes 524288 | tf_op jit(solution)/shard_map/all_to_all | solution.py:11
  155.0 0.2 multiply_reduce_fusion.1
  155.2 13.2 %all_to_all.65 = f32[16,1,128]{2,1,0:T(1,128)S(1)} all-to-all(f32[16,1,128]{2,1,0:T(1,128)S(1)} %broadcast_in_dim.55), channel_id=1, replica_groups=mesh['rows'=16,'x'=4,'y'=8] {'rows'}, dimensions={0} | all-to-all | bytes 16384 | tf_op jit(solution)/shard_map/all_to_all | solution.py:11
  168.4 0.8 multiply_add_fusion
  169.2 0.9 fusion.3
  (31 shorter events, 0.4 us)
Async XLA Ops:
  0.6 62.9 %copy-start = (bf16[512,512]{1,0:T(8,128)(2,1)S(1)}, bf16[512,512]{1,0:T(8,128)(2,1)}, u32[]{:S(2)}) copy-start(bf16[512,512]{1,0:T(8,128)(2,1)} %param.7) | copy-start | bytes 1572868
  0.6 26.8 %copy-start.1 = (bf16[512,256]{1,0:T(8,128)(2,1)S(1)}, bf16[512,256]{1,0:T(8,128)(2,1)}, u32[]{:S(2)}) copy-start(bf16[512,256]{1,0:T(8,128)(2,1)} %param.6) | copy-start | bytes 786436
  27.8 1.0 copy-start.2

commit v5 on v4

v5 whole, which is shorter than its diff:
```python
import jax
import jax.numpy as jnp
from jax import lax
from jax.experimental import pallas as pl
from jax.experimental.pallas import tpu as pltpu
from jax.sharding import Mesh, PartitionSpec as P

RIDGE_WEIGHT = 0.02


def exchanged(tiles, axis):
    return lax.all_to_all(tiles, axis, split_axis=0, concat_axis=0, tiled=True)


def copies_of(value, axis):
    copies = jnp.broadcast_to(value, (lax.axis_size(axis), *value.shape))
    return exchanged(copies, axis)


def per_device(features, targets, centre_points, precond):
    group_rows = float(features.shape[0])
    group_parts = copies_of(features.T, "y")
    gathered = copies_of(group_parts, "x").reshape(-1, features.shape[0])
    gathered, centre_points = lax.optimization_barrier((gathered, centre_points))
    kernel, product = built(centre_points, gathered, targets, group_rows)

    def whole(share, axis):
        return copies_of(share.astype(jnp.bfloat16), axis).reshape(-1, share.shape[1])

    def column_sum(a, b):
        return jnp.sum(a * b, axis=0)

    tiles = product.reshape(lax.axis_size("rows"), -1, product.shape[1])
    residual_share = exchanged(tiles, "rows").astype(jnp.float32).sum(axis=0)
    residual = whole(residual_share, "rows")
    share = features.shape[0] // lax.axis_size(("x", "y"))
    direction, rows_share, (product_now, direction_sq) = stepped(
        precond, residual, kernel, None, share
    )
    rounded = whole(rows_share, ("x", "y"))
    applied_share, rows_sq = returned(kernel, rounded, direction, group_rows, "rows")
    step_size = product_now / (rows_sq / group_rows + RIDGE_WEIGHT * direction_sq)
    residual_share = residual_share - step_size * applied_share
    residual = whole(residual_share, "rows")
    scaled, scaled_rows_share, (product_next, scaled_sq, cross_term) = stepped(
        precond, residual, kernel, direction, share
    )
    momentum = product_next / product_now
    next_sq = scaled_sq + 2.0 * momentum * cross_term + momentum * momentum * direction_sq
    next_rows_share = scaled_rows_share + momentum * rows_share
    known = jnp.stack([step_size, momentum, product_next, next_sq])
    next_rows_share, known = lax.optimization_barrier((next_rows_share, known))
    next_rows = whole(next_rows_share, ("x", "y"))
    next_parts = column_sum(next_rows.astype(jnp.float32), next_rows.astype(jnp.float32))
    row_parts = copies_of(next_parts[None], "rows").reshape(-1, next_parts.shape[-1])
    return finished(row_parts, known, direction, scaled, rounded, next_rows, group_rows)


FAST = pl.BlockSpec(memory_space=pltpu.VMEM)


def built(centre_points, gathered, targets, group_rows):
    feature_count, rows = gathered.shape
    centres = centre_points.shape[0]
    band = centres // 4

    def body(centre_points, gathered, targets, kernel, product):
        gathered_float = gathered[...].astype(jnp.float32)
        squares = jnp.sum(gathered_float * gathered_float, axis=0, keepdims=True)
        row_scale = 1.0 / jnp.sqrt(squares / feature_count + 1e-06)
        for at in range(0, centres, band):
            points = centre_points[at : at + band, :]
            point_float = points.astype(jnp.float32)
            squares = jnp.sum(point_float * point_float, axis=1, keepdims=True)
            centre_scale = 1.0 / jnp.sqrt(squares / feature_count + 1e-06)
            inner = jnp.dot(points, gathered[...], preferred_element_type=jnp.float32)
            cosine = inner * row_scale * centre_scale / feature_count
            values = jnp.exp(8.0 * (cosine - 1.0)).astype(jnp.bfloat16)
            kernel[at : at + band, :] = values
            part = jnp.dot(values, targets[...], preferred_element_type=jnp.float32)
            product[at : at + band, :] = (part / group_rows**0.5).astype(jnp.bfloat16)

    return pl.pallas_call(
        body,
        out_shape=[
            jax.ShapeDtypeStruct((centres, rows), jnp.bfloat16),
            jax.ShapeDtypeStruct((centres, targets.shape[1]), jnp.bfloat16),
        ],
        in_specs=[FAST] * 3,
        out_specs=[FAST] * 2,
        compiler_params=pltpu.CompilerParams(vmem_limit_bytes=12 * 2**20),
        name="built",
    )(centre_points, gathered, targets)


def returned(kernel, rounded, direction, group_rows, axis):
    size = lax.axis_size(axis)
    centres, width = direction.shape
    share = centres // size
    whole_share = share + 2
    part = RIDGE_WEIGHT / size

    def body(kernel, rounded, direction, packed):
        held = rounded[...]
        held_float = held.astype(jnp.float32)
        squares = jnp.sum(held_float * held_float, axis=0, keepdims=True)
        tail = jnp.concatenate([squares, squares], axis=0).astype(jnp.bfloat16)
        product = jnp.dot(kernel[...], held, preferred_element_type=jnp.float32)
        product = (product / group_rows + part * direction[...]).astype(jnp.bfloat16)
        for k in range(size):
            at = k * whole_share
            packed[at : at + share, :] = product[k * share : (k + 1) * share, :]
            packed[at + share : at + whole_share, :] = tail

    packed = pl.pallas_call(
        body,
        out_shape=jax.ShapeDtypeStruct((size * whole_share, width), jnp.bfloat16),
        in_specs=[FAST] * 3,
        out_specs=FAST,
        compiler_params=pltpu.CompilerParams(vmem_limit_bytes=8 * 2**20),
        name="returned",
    )(kernel, rounded, direction)
    arrived = exchanged(packed.reshape(size, whole_share // 2, 2, width), axis)
    total = arrived.astype(jnp.float32).sum(axis=0)
    return total[: share // 2].reshape(-1, width), total[share // 2, 0]


def stepped(precond, residual, kernel, older, share):
    centres, rows = kernel.shape
    width = residual.shape[1]
    size = rows // share
    extra = 2 if older is None else 4
    whole_share = share + extra

    def body(precond, residual, kernel, *rest):
        (scaled_out, packed), olds = rest[-2:], rest[:-2]
        held = residual[...]
        scaled = jnp.dot(precond[...], held, preferred_element_type=jnp.float32)
        scaled_out[...] = scaled
        sums = [
            jnp.sum(held.astype(jnp.float32) * scaled, axis=0, keepdims=True),
            jnp.sum(scaled * scaled, axis=0, keepdims=True),
        ]
        for old in olds:
            sums.append(jnp.sum(scaled * old[...], axis=0, keepdims=True))
            sums.append(sums[0])
        tail = jnp.concatenate(sums, axis=0).astype(jnp.bfloat16)
        product = lax.dot_general(
            kernel[...],
            scaled.astype(jnp.bfloat16),
            (((0,), (0,)), ((), ())),
            preferred_element_type=jnp.float32,
        ).astype(jnp.bfloat16)
        for k in range(size):
            at = k * whole_share
            packed[at : at + share, :] = product[k * share : (k + 1) * share, :]
            packed[at + share : at + whole_share, :] = tail

    operands = [precond, residual, kernel] + ([] if older is None else [older])
    scaled, packed = pl.pallas_call(
        body,
        out_shape=[
            jax.ShapeDtypeStruct((centres, width), jnp.float32),
            jax.ShapeDtypeStruct((size * whole_share, width), jnp.bfloat16),
        ],
        in_specs=[FAST] * len(operands),
        out_specs=[FAST] * 2,
        compiler_params=pltpu.CompilerParams(vmem_limit_bytes=8 * 2**20),
        name="stepped",
    )(*operands)
    arrived = exchanged(packed.reshape(size, whole_share // 2, 2, width), ("x", "y"))
    total = arrived.astype(jnp.float32).sum(axis=0)
    sums = [total[share // 2 + i // 2, i % 2] for i in range(2 if older is None else 3)]
    return scaled, total[: share // 2].reshape(-1, width), sums


def finished(row_parts, known, direction, scaled, rows, next_rows, group_rows):

    def body(parts, known, direction, scaled, rows, next_rows, *rest):
        outputs, held, done = rest[:2], rest[2:4], rest[4]
        rows_sq = jnp.sum(parts[...], axis=0, keepdims=True)
        step_size, momentum = known[0:1, :], known[1:2, :]
        next_step = known[2:3, :] / (rows_sq / group_rows + RIDGE_WEIGHT * known[3:4, :])
        copies = [
            pltpu.make_async_copy(held[i], outputs[i], done.at[i]) for i in range(2)
        ]
        both = rows[...].astype(jnp.float32), next_rows[...].astype(jnp.float32)
        held[1][...] = step_size * both[0] + next_step * both[1]
        copies[1].start()
        old = direction[...]
        held[0][...] = step_size * old + next_step * (scaled[...] + momentum * old)
        copies[0].start()
        copies[1].wait()
        copies[0].wait()

    shapes = [
        jax.ShapeDtypeStruct(direction.shape, jnp.float32),
        jax.ShapeDtypeStruct(rows.shape, jnp.float32),
    ]
    return tuple(
        pl.pallas_call(
            body,
            out_shape=shapes,
            in_specs=[FAST] * 6,
            out_specs=[pl.BlockSpec(memory_space=pl.ANY)] * 2,
            scratch_shapes=[pltpu.VMEM(x.shape, x.dtype) for x in shapes]
            + [pltpu.SemaphoreType.DMA((2,))],
            compiler_params=pltpu.CompilerParams(vmem_limit_bytes=4 * 2**20),
            name="finished",
        )(row_parts, known, direction, scaled, rows, next_rows)
    )


def solution(mesh):
    rows, centres = mesh.devices.shape
    split = Mesh(mesh.devices.reshape(rows, centres // 8, 8), ("rows", "x", "y"))
    plane = ("x", "y")
    return jax.shard_map(
        per_device,
        mesh=split,
        in_specs=(P("rows", plane), P("rows", None), P(plane, None), P(plane, None)),
        out_specs=(P(plane, None), P("rows", None)),
        check_vma=False,
    )
```

time: 171 us -> 169 us (0.988)
  Pallas kernels: 0 us -> 4.5 us
  matrix products: 3.16 us -> 0 us
  other arithmetic: 3.93 us -> 0.85 us
    pallas_call x0 -> x5, Pallas kernels: none -> 4.5 us  [the longest x2 1.77 us: stepped(): pl.pallas_call(body, out_shape=[jax.ShapeDtypeStruct((centres, width), jn...]
    dot_general x7 -> x0, matrix products: 3.16 us -> none  [the longest x2 0.97 us: forward(): jnp.einsum('cr,ct->rt', kernel, values.astype(jnp.bfloat16), preferred_el...]
where the time goes in v5:
time: 169 us; the launch traced here: 168 us
  blocking collectives  161 us (95%)
  Pallas kernels  4.5 us (3%)
    all_to_all x11, blocking collectives, exchanged(): return lax.all_to_all(tiles, axis, split_axis=0, concat_axis=0, tiled=True)  161 us

profile of v5, /device:TPU:1, one launch (start us, length us, event | category | flops | bytes accessed | tf_op | source)
XLA Modules:
  0.0 168.2 jit_solution(12948745786838937759)
XLA Ops:
  0.6 0.7 broadcast_in_dim.24
  1.4 15.4 %all_to_all.55 = bf16[8,8,1024]{2,1,0:T(8,128)(2,1)S(1)} all-to-all(bf16[8,8,1024]{2,1,0:T(8,128)(2,1)S(1)} %broadcast_in_dim.24), channel_id=1, replica_groups=mesh['rows'=16,'x'=4,'y'=8] {'y'}, dimensions={0} | all-to-all | bytes 262144 | tf_op jit(solution)/shard_map/all_to_all | solution.py:12
  16.7 0.1 broadcast_in_dim.25
  16.8 0.0 copy-start.1
  16.8 0.0 copy-start.2
  16.8 10.7 %all_to_all.56 = bf16[4,8,8,1024]{3,2,1,0:T(8,128)(2,1)S(1)} all-to-all(bf16[4,8,8,1024]{3,2,1,0:T(8,128)(2,1)S(1)} %broadcast_in_dim.25), channel_id=1, replica_groups=mesh['rows'=16,'x'=4,'y'=8] {'x'}, dimensions={0} | all-to-all | bytes 1048576 | tf_op jit(solution)/shard_map/all_to_all | solution.py:12
  27.5 0.0 copy-done.1
  27.5 0.0 copy-done.2
  27.5 1.3 built.1
  28.8 0.0 copy-start
  28.8 22.9 %all_to_all.57 = bf16[16,32,128]{2,1,0:T(8,128)(2,1)S(1)} all-to-all(bf16[16,32,128]{2,1,0:T(8,128)(2,1)S(1)} %bitcast.59), channel_id=1, replica_groups=mesh['rows'=16,'x'=4,'y'=8] {'rows'}, dimensions={0} | all-to-all | bytes 262144 | tf_op jit(solution)/shard_map/all_to_all | solution.py:12
  51.8 11.6 %all_to_all.58 = bf16[16,32,128]{2,1,0:T(8,128)(2,1)S(1)} all-to-all(bf16[16,32,128]{2,1,0:T(8,128)(2,1)S(1)} %broadcast_in_dim.26), channel_id=1, replica_groups=mesh['rows'=16,'x'=4,'y'=8] {'rows'}, dimensions={0} | all-to-all | bytes 262144 | tf_op jit(solution)/shard_map/all_to_all | solution.py:12
  63.3 0.0 copy-done
  63.3 0.9 stepped.2
  64.2 13.8 %all_to_all.59 = bf16[32,17,2,128]{3,2,1,0:T(2,128)(2,1)S(1)} all-to-all(bf16[32,17,2,128]{3,2,1,0:T(2,128)(2,1)S(1)} %bitcast.58), channel_id=1, replica_groups=mesh['rows'=16,'x'=4,'y'=8] {'x','y'}, dimensions={0} | all-to-all | bytes 557056 | tf_op jit(solution)/shard_map/all_to_all | solution.py:12
  78.0 0.2 convert_reduce_fusion.1
  78.3 15.9 %all_to_all.60 = bf16[32,32,128]{2,1,0:T(8,128)(2,1)S(1)} all-to-all(bf16[32,32,128]{2,1,0:T(8,128)(2,1)S(1)} %broadcast_in_dim.27), channel_id=1, replica_groups=mesh['rows'=16,'x'=4,'y'=8] {'x','y'}, dimensions={0} | all-to-all | bytes 524288 | tf_op jit(solution)/shard_map/all_to_all | solution.py:12
  94.2 0.4 returned.1
  94.6 15.5 %all_to_all.61 = bf16[16,17,2,128]{3,2,1,0:T(2,128)(2,1)S(1)} all-to-all(bf16[16,17,2,128]{3,2,1,0:T(2,128)(2,1)S(1)} %bitcast.54), channel_id=1, replica_groups=mesh['rows'=16,'x'=4,'y'=8] {'rows'}, dimensions={0} | all-to-all | bytes 278528 | tf_op jit(solution)/shard_map/all_to_all | solution.py:12
  110.1 0.1 convert_reduce_fusion.2
  110.3 11.3 %all_to_all.62 = bf16[16,32,128]{2,1,0:T(8,128)(2,1)S(1)} all-to-all(bf16[16,32,128]{2,1,0:T(8,128)(2,1)S(1)} %broadcast_in_dim.28), channel_id=1, replica_groups=mesh['rows'=16,'x'=4,'y'=8] {'rows'}, dimensions={0} | all-to-all | bytes 262144 | tf_op jit(solution)/shard_map/all_to_all | solution.py:12
  121.6 0.9 stepped.3
  122.5 14.6 %all_to_all.63 = bf16[32,18,2,128]{3,2,1,0:T(2,128)(2,1)S(1)} all-to-all(bf16[32,18,2,128]{3,2,1,0:T(2,128)(2,1)S(1)} %bitcast.57), channel_id=1, replica_groups=mesh['rows'=16,'x'=4,'y'=8] {'x','y'}, dimensions={0} | all-to-all | bytes 589824 | tf_op jit(solution)/shard_map/all_to_all | solution.py:12
  137.1 0.2 convert_reduce_fusion
  137.5 16.3 %all_to_all.64 = bf16[32,32,128]{2,1,0:T(8,128)(2,1)S(1)} all-to-all(bf16[32,32,128]{2,1,0:T(8,128)(2,1)S(1)} %broadcast_in_dim.29), channel_id=1, replica_groups=mesh['rows'=16,'x'=4,'y'=8] {'x','y'}, dimensions={0} | all-to-all | bytes 524288 | tf_op jit(solution)/shard_map/all_to_all | solution.py:12
  153.8 0.2 multiply_reduce_fusion
  154.0 13.2 %all_to_all.65 = f32[16,1,128]{2,1,0:T(1,128)S(1)} all-to-all(f32[16,1,128]{2,1,0:T(1,128)S(1)} %broadcast_in_dim.30), channel_id=1, replica_groups=mesh['rows'=16,'x'=4,'y'=8] {'rows'}, dimensions={0} | all-to-all | bytes 16384 | tf_op jit(solution)/shard_map/all_to_all | solution.py:12
  167.2 1.0 finished.1
  (17 shorter events, 0.2 us)
Async XLA Ops:
  16.8 10.7 %copy-start.1 = (bf16[512,256]{1,0:T(8,128)(2,1)S(1)}, bf16[512,256]{1,0:T(8,128)(2,1)}, u32[]{:S(2)}) copy-start(bf16[512,256]{1,0:T(8,128)(2,1)} %centre_points) | copy-start | bytes 786436
  16.8 10.7 %copy-start.2 = (bf16[1024,128]{1,0:T(8,128)(2,1)S(1)}, bf16[1024,128]{1,0:T(8,128)(2,1)}, u32[]{:S(2)}) copy-start(bf16[1024,128]{1,0:T(8,128)(2,1)} %targets.1) | copy-start | bytes 786436
  28.8 34.5 %copy-start = (bf16[512,512]{1,0:T(8,128)(2,1)S(1)}, bf16[512,512]{1,0:T(8,128)(2,1)}, u32[]{:S(2)}) copy-start(bf16[512,512]{1,0:T(8,128)(2,1)} %precond.3) | copy-start | bytes 1572868

commit v6 on v5

--- a/solution.py
+++ b/solution.py
@@ -6,6 +6,7 @@
 from jax.sharding import Mesh, PartitionSpec as P
 
 RIDGE_WEIGHT = 0.02
+ROWS = ("core", "z")
 
 
 def exchanged(tiles, axis):
@@ -30,18 +31,18 @@
     def column_sum(a, b):
         return jnp.sum(a * b, axis=0)
 
-    tiles = product.reshape(lax.axis_size("rows"), -1, product.shape[1])
-    residual_share = exchanged(tiles, "rows").astype(jnp.float32).sum(axis=0)
-    residual = whole(residual_share, "rows")
+    tiles = product.reshape(lax.axis_size(ROWS), -1, product.shape[1])
+    residual_share = exchanged(tiles, ROWS).astype(jnp.float32).sum(axis=0)
+    residual = whole(residual_share, ROWS)
     share = features.shape[0] // lax.axis_size(("x", "y"))
     direction, rows_share, (product_now, direction_sq) = stepped(
         precond, residual, kernel, None, share
     )
-    rounded = whole(rows_share, ("x", "y"))
-    applied_share, rows_sq = returned(kernel, rounded, direction, group_rows, "rows")
+    rounded = whole(rows_share, ("y", "x"))
+    applied_share, rows_sq = returned(kernel, rounded, direction, group_rows, ROWS)
     step_size = product_now / (rows_sq / group_rows + RIDGE_WEIGHT * direction_sq)
     residual_share = residual_share - step_size * applied_share
-    residual = whole(residual_share, "rows")
+    residual = whole(residual_share, ROWS)
     scaled, scaled_rows_share, (product_next, scaled_sq, cross_term) = stepped(
         precond, residual, kernel, direction, share
     )
@@ -50,9 +51,9 @@
     next_rows_share = scaled_rows_share + momentum * rows_share
     known = jnp.stack([step_size, momentum, product_next, next_sq])
     next_rows_share, known = lax.optimization_barrier((next_rows_share, known))
-    next_rows = whole(next_rows_share, ("x", "y"))
+    next_rows = whole(next_rows_share, ("y", "x"))
     next_parts = column_sum(next_rows.astype(jnp.float32), next_rows.astype(jnp.float32))
-    row_parts = copies_of(next_parts[None], "rows").reshape(-1, next_parts.shape[-1])
+    row_parts = copies_of(next_parts[None], ROWS).reshape(-1, next_parts.shape[-1])
     return finished(row_parts, known, direction, scaled, rounded, next_rows, group_rows)
 
 
@@ -168,7 +169,7 @@
         compiler_params=pltpu.CompilerParams(vmem_limit_bytes=8 * 2**20),
         name="stepped",
     )(*operands)
-    arrived = exchanged(packed.reshape(size, whole_share // 2, 2, width), ("x", "y"))
+    arrived = exchanged(packed.reshape(size, whole_share // 2, 2, width), ("y", "x"))
     total = arrived.astype(jnp.float32).sum(axis=0)
     sums = [total[share // 2 + i // 2, i % 2] for i in range(2 if older is None else 3)]
     return scaled, total[: share // 2].reshape(-1, width), sums
@@ -213,12 +214,13 @@
 
 def solution(mesh):
     rows, centres = mesh.devices.shape
-    split = Mesh(mesh.devices.reshape(rows, centres // 8, 8), ("rows", "x", "y"))
+    split = Mesh(mesh.devices.reshape(rows // 2, 2, centres // 8, 8), ("z", "core", "x", "y"))
+    held = ("z", "core")
     plane = ("x", "y")
     return jax.shard_map(
         per_device,
         mesh=split,
-        in_specs=(P("rows", plane), P("rows", None), P(plane, None), P(plane, None)),
-        out_specs=(P(plane, None), P("rows", None)),
+        in_specs=(P(held, plane), P(held, None), P(plane, None), P(plane, None)),
+        out_specs=(P(plane, None), P(held, None)),
         check_vma=False,
     )

time: 169 us -> 167 us (0.988)
  blocking collectives: 161 us -> 159 us
    all_to_all x11, blocking collectives: 161 us -> 159 us  [exchanged(): return lax.all_to_all(tiles, axis, split_axis=0, concat_axis=0, tiled=True)]
where the time goes in v6:
time: 167 us; the launch traced here: 166 us
  blocking collectives  159 us (95%)
  Pallas kernels  4.5 us (3%)
    all_to_all x11, blocking collectives, exchanged(): return lax.all_to_all(tiles, axis, split_axis=0, concat_axis=0, tiled=True)  159 us

profile of v6, /device:TPU:1, one launch (start us, length us, event | category | flops | bytes accessed | tf_op | source)
XLA Modules:
  0.0 166.3 jit_solution(8596424782126551854)
XLA Ops:
  0.6 0.7 broadcast_in_dim.24
  1.4 15.4 %all_to_all.55 = bf16[8,8,1024]{2,1,0:T(8,128)(2,1)S(1)} all-to-all(bf16[8,8,1024]{2,1,0:T(8,128)(2,1)S(1)} %broadcast_in_dim.24), channel_id=1, replica_groups=mesh['z'=8,'core'=2,'x'=4,'y'=8] {'y'}, dimensions={0} | all-to-all | bytes 262144 | tf_op jit(solution)/shard_map/all_to_all | solution.py:13
  16.7 0.1 broadcast_in_dim.25
  16.8 0.0 copy-start.1
  16.8 0.0 copy-start.2
  16.8 10.7 %all_to_all.56 = bf16[4,8,8,1024]{3,2,1,0:T(8,128)(2,1)S(1)} all-to-all(bf16[4,8,8,1024]{3,2,1,0:T(8,128)(2,1)S(1)} %broadcast_in_dim.25), channel_id=1, replica_groups=mesh['z'=8,'core'=2,'x'=4,'y'=8] {'x'}, dimensions={0} | all-to-all | bytes 1048576 | tf_op jit(solution)/shard_map/all_to_all | solution.py:13
  27.5 0.0 copy-done.1
  27.5 0.0 copy-done.2
  27.5 1.3 built.1
  28.8 0.0 copy-start
  28.8 21.4 %all_to_all.57 = bf16[16,32,128]{2,1,0:T(8,128)(2,1)S(1)} all-to-all(bf16[16,32,128]{2,1,0:T(8,128)(2,1)S(1)} %bitcast.59), channel_id=1, replica_groups=mesh['z'=8,'core'=2,'x'=4,'y'=8] {'core','z'}, dimensions={0} | all-to-all | bytes 262144 | tf_op jit(solution)/shard_map/all_to_all | solution.py:13
  50.3 11.6 %all_to_all.58 = bf16[16,32,128]{2,1,0:T(8,128)(2,1)S(1)} all-to-all(bf16[16,32,128]{2,1,0:T(8,128)(2,1)S(1)} %broadcast_in_dim.26), channel_id=1, replica_groups=mesh['z'=8,'core'=2,'x'=4,'y'=8] {'core','z'}, dimensions={0} | all-to-all | bytes 262144 | tf_op jit(solution)/shard_map/all_to_all | solution.py:13
  61.8 0.0 copy-done
  61.8 0.9 stepped.2
  62.7 13.7 %all_to_all.59 = bf16[32,17,2,128]{3,2,1,0:T(2,128)(2,1)S(1)} all-to-all(bf16[32,17,2,128]{3,2,1,0:T(2,128)(2,1)S(1)} %bitcast.58), channel_id=1, replica_groups=mesh['z'=8,'core'=2,'x'=4,'y'=8] {'y','x'}, dimensions={0} | all-to-all | bytes 557056 | tf_op jit(solution)/shard_map/all_to_all | solution.py:13
  76.4 0.2 convert_reduce_fusion.1
  76.7 15.5 %all_to_all.60 = bf16[32,32,128]{2,1,0:T(8,128)(2,1)S(1)} all-to-all(bf16[32,32,128]{2,1,0:T(8,128)(2,1)S(1)} %broadcast_in_dim.27), channel_id=1, replica_groups=mesh['z'=8,'core'=2,'x'=4,'y'=8] {'y','x'}, dimensions={0} | all-to-all | bytes 524288 | tf_op jit(solution)/shard_map/all_to_all | solution.py:13
  92.2 0.4 returned.1
  92.7 14.9 %all_to_all.61 = bf16[16,17,2,128]{3,2,1,0:T(2,128)(2,1)S(1)} all-to-all(bf16[16,17,2,128]{3,2,1,0:T(2,128)(2,1)S(1)} %bitcast.54), channel_id=1, replica_groups=mesh['z'=8,'core'=2,'x'=4,'y'=8] {'core','z'}, dimensions={0} | all-to-all | bytes 278528 | tf_op jit(solution)/shard_map/all_to_all | solution.py:13
  107.6 0.1 convert_reduce_fusion.2
  107.8 11.7 %all_to_all.62 = bf16[16,32,128]{2,1,0:T(8,128)(2,1)S(1)} all-to-all(bf16[16,32,128]{2,1,0:T(8,128)(2,1)S(1)} %broadcast_in_dim.28), channel_id=1, replica_groups=mesh['z'=8,'core'=2,'x'=4,'y'=8] {'core','z'}, dimensions={0} | all-to-all | bytes 262144 | tf_op jit(solution)/shard_map/all_to_all | solution.py:13
  119.5 0.9 stepped.3
  120.4 14.1 %all_to_all.63 = bf16[32,18,2,128]{3,2,1,0:T(2,128)(2,1)S(1)} all-to-all(bf16[32,18,2,128]{3,2,1,0:T(2,128)(2,1)S(1)} %bitcast.57), channel_id=1, replica_groups=mesh['z'=8,'core'=2,'x'=4,'y'=8] {'y','x'}, dimensions={0} | all-to-all | bytes 589824 | tf_op jit(solution)/shard_map/all_to_all | solution.py:13
  134.5 0.2 convert_reduce_fusion
  134.9 15.8 %all_to_all.64 = bf16[32,32,128]{2,1,0:T(8,128)(2,1)S(1)} all-to-all(bf16[32,32,128]{2,1,0:T(8,128)(2,1)S(1)} %broadcast_in_dim.29), channel_id=1, replica_groups=mesh['z'=8,'core'=2,'x'=4,'y'=8] {'y','x'}, dimensions={0} | all-to-all | bytes 524288 | tf_op jit(solution)/shard_map/all_to_all | solution.py:13
  150.7 0.2 multiply_reduce_fusion
  150.8 14.4 %all_to_all.65 = f32[16,1,128]{2,1,0:T(1,128)S(1)} all-to-all(f32[16,1,128]{2,1,0:T(1,128)S(1)} %broadcast_in_dim.30), channel_id=1, replica_groups=mesh['z'=8,'core'=2,'x'=4,'y'=8] {'core','z'}, dimensions={0} | all-to-all | bytes 16384 | tf_op jit(solution)/shard_map/all_to_all | solution.py:13
  165.3 1.0 finished.1
  (17 shorter events, 0.2 us)
Async XLA Ops:
  16.8 10.7 %copy-start.1 = (bf16[512,256]{1,0:T(8,128)(2,1)S(1)}, bf16[512,256]{1,0:T(8,128)(2,1)}, u32[]{:S(2)}) copy-start(bf16[512,256]{1,0:T(8,128)(2,1)} %centre_points) | copy-start | bytes 786436
  16.8 10.7 %copy-start.2 = (bf16[1024,128]{1,0:T(8,128)(2,1)S(1)}, bf16[1024,128]{1,0:T(8,128)(2,1)}, u32[]{:S(2)}) copy-start(bf16[1024,128]{1,0:T(8,128)(2,1)} %targets.1) | copy-start | bytes 786436
  28.8 33.0 %copy-start = (bf16[512,512]{1,0:T(8,128)(2,1)S(1)}, bf16[512,512]{1,0:T(8,128)(2,1)}, u32[]{:S(2)}) copy-start(bf16[512,512]{1,0:T(8,128)(2,1)} %precond.3) | copy-start | bytes 1572868

commit v7 on v6

--- a/solution.py
+++ b/solution.py
@@ -1,3 +1,5 @@
+import math
+
 import jax
 import jax.numpy as jnp
 from jax import lax
@@ -6,6 +8,7 @@
 from jax.sharding import Mesh, PartitionSpec as P
 
 RIDGE_WEIGHT = 0.02
+SHARP = 8.0 * math.log2(math.e)
 ROWS = ("core", "z")
 
 
@@ -63,7 +66,7 @@
 def built(centre_points, gathered, targets, group_rows):
     feature_count, rows = gathered.shape
     centres = centre_points.shape[0]
-    band = centres // 4
+    band = centres // 2
 
     def body(centre_points, gathered, targets, kernel, product):
         gathered_float = gathered[...].astype(jnp.float32)
@@ -73,10 +76,9 @@
             points = centre_points[at : at + band, :]
             point_float = points.astype(jnp.float32)
             squares = jnp.sum(point_float * point_float, axis=1, keepdims=True)
-            centre_scale = 1.0 / jnp.sqrt(squares / feature_count + 1e-06)
+            centre_scale = (SHARP / feature_count) / jnp.sqrt(squares / feature_count + 1e-06)
             inner = jnp.dot(points, gathered[...], preferred_element_type=jnp.float32)
-            cosine = inner * row_scale * centre_scale / feature_count
-            values = jnp.exp(8.0 * (cosine - 1.0)).astype(jnp.bfloat16)
+            values = jnp.exp2(inner * row_scale * centre_scale - SHARP).astype(jnp.bfloat16)
             kernel[at : at + band, :] = values
             part = jnp.dot(values, targets[...], preferred_element_type=jnp.float32)
             product[at : at + band, :] = (part / group_rows**0.5).astype(jnp.bfloat16)

time: 167 us -> 166 us (level)
  no operation moved by 1% of the time
where the time goes in v7:
time: 166 us
  blocking collectives  159 us (96%)
  Pallas kernels  4.12 us (2%)
    all_to_all x11, blocking collectives, exchanged(): return lax.all_to_all(tiles, axis, split_axis=0, concat_axis=0, tiled=True)  159 us

profile of v7, /device:TPU:1, one launch (start us, length us, event | category | flops | bytes accessed | tf_op | source)
XLA Modules:
  0.0 165.9 jit_solution(6457995693956434534)
XLA Ops:
  0.6 0.7 broadcast_in_dim.24
  1.4 15.4 %all_to_all.55 = bf16[8,8,1024]{2,1,0:T(8,128)(2,1)S(1)} all-to-all(bf16[8,8,1024]{2,1,0:T(8,128)(2,1)S(1)} %broadcast_in_dim.24), channel_id=1, replica_groups=mesh['z'=8,'core'=2,'x'=4,'y'=8] {'y'}, dimensions={0} | all-to-all | bytes 262144 | tf_op jit(solution)/shard_map/all_to_all | solution.py:16
  16.7 0.1 broadcast_in_dim.25
  16.8 0.0 copy-start.1
  16.8 0.0 copy-start.2
  16.8 10.7 %all_to_all.56 = bf16[4,8,8,1024]{3,2,1,0:T(8,128)(2,1)S(1)} all-to-all(bf16[4,8,8,1024]{3,2,1,0:T(8,128)(2,1)S(1)} %broadcast_in_dim.25), channel_id=1, replica_groups=mesh['z'=8,'core'=2,'x'=4,'y'=8] {'x'}, dimensions={0} | all-to-all | bytes 1048576 | tf_op jit(solution)/shard_map/all_to_all | solution.py:16
  27.5 0.0 copy-done.1
  27.5 0.0 copy-done.2
  27.5 0.9 built.1
  28.4 0.0 copy-start
  28.5 21.4 %all_to_all.57 = bf16[16,32,128]{2,1,0:T(8,128)(2,1)S(1)} all-to-all(bf16[16,32,128]{2,1,0:T(8,128)(2,1)S(1)} %bitcast.59), channel_id=1, replica_groups=mesh['z'=8,'core'=2,'x'=4,'y'=8] {'core','z'}, dimensions={0} | all-to-all | bytes 262144 | tf_op jit(solution)/shard_map/all_to_all | solution.py:16
  49.9 11.6 %all_to_all.58 = bf16[16,32,128]{2,1,0:T(8,128)(2,1)S(1)} all-to-all(bf16[16,32,128]{2,1,0:T(8,128)(2,1)S(1)} %broadcast_in_dim.26), channel_id=1, replica_groups=mesh['z'=8,'core'=2,'x'=4,'y'=8] {'core','z'}, dimensions={0} | all-to-all | bytes 262144 | tf_op jit(solution)/shard_map/all_to_all | solution.py:16
  61.4 0.0 copy-done
  61.4 0.9 stepped.2
  62.3 13.7 %all_to_all.59 = bf16[32,17,2,128]{3,2,1,0:T(2,128)(2,1)S(1)} all-to-all(bf16[32,17,2,128]{3,2,1,0:T(2,128)(2,1)S(1)} %bitcast.58), channel_id=1, replica_groups=mesh['z'=8,'core'=2,'x'=4,'y'=8] {'y','x'}, dimensions={0} | all-to-all | bytes 557056 | tf_op jit(solution)/shard_map/all_to_all | solution.py:16
  76.1 0.2 convert_reduce_fusion.1
  76.4 15.5 %all_to_all.60 = bf16[32,32,128]{2,1,0:T(8,128)(2,1)S(1)} all-to-all(bf16[32,32,128]{2,1,0:T(8,128)(2,1)S(1)} %broadcast_in_dim.27), channel_id=1, replica_groups=mesh['z'=8,'core'=2,'x'=4,'y'=8] {'y','x'}, dimensions={0} | all-to-all | bytes 524288 | tf_op jit(solution)/shard_map/all_to_all | solution.py:16
  91.9 0.4 returned.1
  92.3 14.9 %all_to_all.61 = bf16[16,17,2,128]{3,2,1,0:T(2,128)(2,1)S(1)} all-to-all(bf16[16,17,2,128]{3,2,1,0:T(2,128)(2,1)S(1)} %bitcast.54), channel_id=1, replica_groups=mesh['z'=8,'core'=2,'x'=4,'y'=8] {'core','z'}, dimensions={0} | all-to-all | bytes 278528 | tf_op jit(solution)/shard_map/all_to_all | solution.py:16
  107.2 0.1 convert_reduce_fusion.2
  107.4 11.7 %all_to_all.62 = bf16[16,32,128]{2,1,0:T(8,128)(2,1)S(1)} all-to-all(bf16[16,32,128]{2,1,0:T(8,128)(2,1)S(1)} %broadcast_in_dim.28), channel_id=1, replica_groups=mesh['z'=8,'core'=2,'x'=4,'y'=8] {'core','z'}, dimensions={0} | all-to-all | bytes 262144 | tf_op jit(solution)/shard_map/all_to_all | solution.py:16
  119.1 0.9 stepped.3
  120.0 14.1 %all_to_all.63 = bf16[32,18,2,128]{3,2,1,0:T(2,128)(2,1)S(1)} all-to-all(bf16[32,18,2,128]{3,2,1,0:T(2,128)(2,1)S(1)} %bitcast.57), channel_id=1, replica_groups=mesh['z'=8,'core'=2,'x'=4,'y'=8] {'y','x'}, dimensions={0} | all-to-all | bytes 589824 | tf_op jit(solution)/shard_map/all_to_all | solution.py:16
  134.1 0.2 convert_reduce_fusion
  134.5 15.8 %all_to_all.64 = bf16[32,32,128]{2,1,0:T(8,128)(2,1)S(1)} all-to-all(bf16[32,32,128]{2,1,0:T(8,128)(2,1)S(1)} %broadcast_in_dim.29), channel_id=1, replica_groups=mesh['z'=8,'core'=2,'x'=4,'y'=8] {'y','x'}, dimensions={0} | all-to-all | bytes 524288 | tf_op jit(solution)/shard_map/all_to_all | solution.py:16
  150.3 0.2 multiply_reduce_fusion
  150.5 14.4 %all_to_all.65 = f32[16,1,128]{2,1,0:T(1,128)S(1)} all-to-all(f32[16,1,128]{2,1,0:T(1,128)S(1)} %broadcast_in_dim.30), channel_id=1, replica_groups=mesh['z'=8,'core'=2,'x'=4,'y'=8] {'core','z'}, dimensions={0} | all-to-all | bytes 16384 | tf_op jit(solution)/shard_map/all_to_all | solution.py:16
  164.9 1.0 finished.1
  (17 shorter events, 0.2 us)
Async XLA Ops:
  16.8 10.7 %copy-start.1 = (bf16[512,256]{1,0:T(8,128)(2,1)S(1)}, bf16[512,256]{1,0:T(8,128)(2,1)}, u32[]{:S(2)}) copy-start(bf16[512,256]{1,0:T(8,128)(2,1)} %centre_points) | copy-start | bytes 786436
  16.8 10.7 %copy-start.2 = (bf16[1024,128]{1,0:T(8,128)(2,1)S(1)}, bf16[1024,128]{1,0:T(8,128)(2,1)}, u32[]{:S(2)}) copy-start(bf16[1024,128]{1,0:T(8,128)(2,1)} %targets.1) | copy-start | bytes 786436
  28.4 33.0 %copy-start = (bf16[512,512]{1,0:T(8,128)(2,1)S(1)}, bf16[512,512]{1,0:T(8,128)(2,1)}, u32[]{:S(2)}) copy-start(bf16[512,512]{1,0:T(8,128)(2,1)} %precond.3) | copy-start | bytes 1572868

commit v8 on v7

--- a/solution.py
+++ b/solution.py
@@ -66,22 +66,20 @@
 def built(centre_points, gathered, targets, group_rows):
     feature_count, rows = gathered.shape
     centres = centre_points.shape[0]
-    band = centres // 2
 
     def body(centre_points, gathered, targets, kernel, product):
         gathered_float = gathered[...].astype(jnp.float32)
         squares = jnp.sum(gathered_float * gathered_float, axis=0, keepdims=True)
         row_scale = 1.0 / jnp.sqrt(squares / feature_count + 1e-06)
-        for at in range(0, centres, band):
-            points = centre_points[at : at + band, :]
-            point_float = points.astype(jnp.float32)
-            squares = jnp.sum(point_float * point_float, axis=1, keepdims=True)
-            centre_scale = (SHARP / feature_count) / jnp.sqrt(squares / feature_count + 1e-06)
-            inner = jnp.dot(points, gathered[...], preferred_element_type=jnp.float32)
-            values = jnp.exp2(inner * row_scale * centre_scale - SHARP).astype(jnp.bfloat16)
-            kernel[at : at + band, :] = values
-            part = jnp.dot(values, targets[...], preferred_element_type=jnp.float32)
-            product[at : at + band, :] = (part / group_rows**0.5).astype(jnp.bfloat16)
+        points = centre_points[...]
+        point_float = points.astype(jnp.float32)
+        squares = jnp.sum(point_float * point_float, axis=1, keepdims=True)
+        centre_scale = (SHARP / feature_count) / jnp.sqrt(squares / feature_count + 1e-06)
+        inner = jnp.dot(points, gathered[...], preferred_element_type=jnp.float32)
+        values = jnp.exp2(inner * row_scale * centre_scale - SHARP).astype(jnp.bfloat16)
+        kernel[...] = values
+        part = jnp.dot(values, targets[...], preferred_element_type=jnp.float32)
+        product[...] = (part / group_rows**0.5).astype(jnp.bfloat16)
 
     return pl.pallas_call(
         body,

time: 166 us -> 166 us (level)
  no operation moved by 1% of the time
where the time goes in v8:
time: 166 us
  blocking collectives  159 us (96%)
  Pallas kernels  4.05 us (2%)
    all_to_all x11, blocking collectives, exchanged(): return lax.all_to_all(tiles, axis, split_axis=0, concat_axis=0, tiled=True)  159 us

profile of v8, /device:TPU:1, one launch (start us, length us, event | category | flops | bytes accessed | tf_op | source)
XLA Modules:
  0.0 165.8 jit_solution(14147395349940837819)
XLA Ops:
  0.6 0.7 broadcast_in_dim.24
  1.4 15.4 %all_to_all.55 = bf16[8,8,1024]{2,1,0:T(8,128)(2,1)S(1)} all-to-all(bf16[8,8,1024]{2,1,0:T(8,128)(2,1)S(1)} %broadcast_in_dim.24), channel_id=1, replica_groups=mesh['z'=8,'core'=2,'x'=4,'y'=8] {'y'}, dimensions={0} | all-to-all | bytes 262144 | tf_op jit(solution)/shard_map/all_to_all | solution.py:16
  16.7 0.1 broadcast_in_dim.25
  16.8 0.0 copy-start.1
  16.8 0.0 copy-start.2
  16.8 10.7 %all_to_all.56 = bf16[4,8,8,1024]{3,2,1,0:T(8,128)(2,1)S(1)} all-to-all(bf16[4,8,8,1024]{3,2,1,0:T(8,128)(2,1)S(1)} %broadcast_in_dim.25), channel_id=1, replica_groups=mesh['z'=8,'core'=2,'x'=4,'y'=8] {'x'}, dimensions={0} | all-to-all | bytes 1048576 | tf_op jit(solution)/shard_map/all_to_all | solution.py:16
  27.5 0.0 copy-done.1
  27.5 0.0 copy-done.2
  27.5 0.8 built.1
  28.4 0.0 copy-start
  28.4 21.4 %all_to_all.57 = bf16[16,32,128]{2,1,0:T(8,128)(2,1)S(1)} all-to-all(bf16[16,32,128]{2,1,0:T(8,128)(2,1)S(1)} %bitcast.59), channel_id=1, replica_groups=mesh['z'=8,'core'=2,'x'=4,'y'=8] {'core','z'}, dimensions={0} | all-to-all | bytes 262144 | tf_op jit(solution)/shard_map/all_to_all | solution.py:16
  49.8 11.6 %all_to_all.58 = bf16[16,32,128]{2,1,0:T(8,128)(2,1)S(1)} all-to-all(bf16[16,32,128]{2,1,0:T(8,128)(2,1)S(1)} %broadcast_in_dim.26), channel_id=1, replica_groups=mesh['z'=8,'core'=2,'x'=4,'y'=8] {'core','z'}, dimensions={0} | all-to-all | bytes 262144 | tf_op jit(solution)/shard_map/all_to_all | solution.py:16
  61.4 0.0 copy-done
  61.4 0.9 stepped.2
  62.3 13.7 %all_to_all.59 = bf16[32,17,2,128]{3,2,1,0:T(2,128)(2,1)S(1)} all-to-all(bf16[32,17,2,128]{3,2,1,0:T(2,128)(2,1)S(1)} %bitcast.58), channel_id=1, replica_groups=mesh['z'=8,'core'=2,'x'=4,'y'=8] {'y','x'}, dimensions={0} | all-to-all | bytes 557056 | tf_op jit(solution)/shard_map/all_to_all | solution.py:16
  76.0 0.2 convert_reduce_fusion.1
  76.3 15.5 %all_to_all.60 = bf16[32,32,128]{2,1,0:T(8,128)(2,1)S(1)} all-to-all(bf16[32,32,128]{2,1,0:T(8,128)(2,1)S(1)} %broadcast_in_dim.27), channel_id=1, replica_groups=mesh['z'=8,'core'=2,'x'=4,'y'=8] {'y','x'}, dimensions={0} | all-to-all | bytes 524288 | tf_op jit(solution)/shard_map/all_to_all | solution.py:16
  91.8 0.4 returned.1
  92.2 14.9 %all_to_all.61 = bf16[16,17,2,128]{3,2,1,0:T(2,128)(2,1)S(1)} all-to-all(bf16[16,17,2,128]{3,2,1,0:T(2,128)(2,1)S(1)} %bitcast.54), channel_id=1, replica_groups=mesh['z'=8,'core'=2,'x'=4,'y'=8] {'core','z'}, dimensions={0} | all-to-all | bytes 278528 | tf_op jit(solution)/shard_map/all_to_all | solution.py:16
  107.1 0.1 convert_reduce_fusion.2
  107.3 11.7 %all_to_all.62 = bf16[16,32,128]{2,1,0:T(8,128)(2,1)S(1)} all-to-all(bf16[16,32,128]{2,1,0:T(8,128)(2,1)S(1)} %broadcast_in_dim.28), channel_id=1, replica_groups=mesh['z'=8,'core'=2,'x'=4,'y'=8] {'core','z'}, dimensions={0} | all-to-all | bytes 262144 | tf_op jit(solution)/shard_map/all_to_all | solution.py:16
  119.0 0.9 stepped.3
  119.9 14.1 %all_to_all.63 = bf16[32,18,2,128]{3,2,1,0:T(2,128)(2,1)S(1)} all-to-all(bf16[32,18,2,128]{3,2,1,0:T(2,128)(2,1)S(1)} %bitcast.57), channel_id=1, replica_groups=mesh['z'=8,'core'=2,'x'=4,'y'=8] {'y','x'}, dimensions={0} | all-to-all | bytes 589824 | tf_op jit(solution)/shard_map/all_to_all | solution.py:16
  134.0 0.2 convert_reduce_fusion
  134.4 15.8 %all_to_all.64 = bf16[32,32,128]{2,1,0:T(8,128)(2,1)S(1)} all-to-all(bf16[32,32,128]{2,1,0:T(8,128)(2,1)S(1)} %broadcast_in_dim.29), channel_id=1, replica_groups=mesh['z'=8,'core'=2,'x'=4,'y'=8] {'y','x'}, dimensions={0} | all-to-all | bytes 524288 | tf_op jit(solution)/shard_map/all_to_all | solution.py:16
  150.2 0.2 multiply_reduce_fusion
  150.4 14.4 %all_to_all.65 = f32[16,1,128]{2,1,0:T(1,128)S(1)} all-to-all(f32[16,1,128]{2,1,0:T(1,128)S(1)} %broadcast_in_dim.30), channel_id=1, replica_groups=mesh['z'=8,'core'=2,'x'=4,'y'=8] {'core','z'}, dimensions={0} | all-to-all | bytes 16384 | tf_op jit(solution)/shard_map/all_to_all | solution.py:16
  164.8 1.0 finished.1
  (17 shorter events, 0.2 us)
Async XLA Ops:
  16.8 10.7 %copy-start.1 = (bf16[512,256]{1,0:T(8,128)(2,1)S(1)}, bf16[512,256]{1,0:T(8,128)(2,1)}, u32[]{:S(2)}) copy-start(bf16[512,256]{1,0:T(8,128)(2,1)} %centre_points) | copy-start | bytes 786436
  16.8 10.7 %copy-start.2 = (bf16[1024,128]{1,0:T(8,128)(2,1)S(1)}, bf16[1024,128]{1,0:T(8,128)(2,1)}, u32[]{:S(2)}) copy-start(bf16[1024,128]{1,0:T(8,128)(2,1)} %targets.1) | copy-start | bytes 786436
  28.4 33.0 %copy-start = (bf16[512,512]{1,0:T(8,128)(2,1)S(1)}, bf16[512,512]{1,0:T(8,128)(2,1)}, u32[]{:S(2)}) copy-start(bf16[512,512]{1,0:T(8,128)(2,1)} %precond.3) | copy-start | bytes 1572868

commit v9 on v7

--- a/solution.py
+++ b/solution.py
@@ -184,17 +184,23 @@
         rows_sq = jnp.sum(parts[...], axis=0, keepdims=True)
         step_size, momentum = known[0:1, :], known[1:2, :]
         next_step = known[2:3, :] / (rows_sq / group_rows + RIDGE_WEIGHT * known[3:4, :])
-        copies = [
-            pltpu.make_async_copy(held[i], outputs[i], done.at[i]) for i in range(2)
-        ]
-        both = rows[...].astype(jnp.float32), next_rows[...].astype(jnp.float32)
-        held[1][...] = step_size * both[0] + next_step * both[1]
-        copies[1].start()
+        copies = [pltpu.make_async_copy(held[0], outputs[0], done.at[0])]
+        half = rows.shape[0] // 2
+        for i in range(2):
+            part = pl.ds(i * half, half)
+            both = rows[part, :].astype(jnp.float32), next_rows[part, :].astype(jnp.float32)
+            held[1][part, :] = step_size * both[0] + next_step * both[1]
+            copies.append(
+                pltpu.make_async_copy(
+                    held[1].at[part, :], outputs[1].at[part, :], done.at[i + 1]
+                )
+            )
+            copies[-1].start()
         old = direction[...]
         held[0][...] = step_size * old + next_step * (scaled[...] + momentum * old)
         copies[0].start()
-        copies[1].wait()
-        copies[0].wait()
+        for copy in copies:
+            copy.wait()
 
     shapes = [
         jax.ShapeDtypeStruct(direction.shape, jnp.float32),
@@ -207,7 +213,7 @@
             in_specs=[FAST] * 6,
             out_specs=[pl.BlockSpec(memory_space=pl.ANY)] * 2,
             scratch_shapes=[pltpu.VMEM(x.shape, x.dtype) for x in shapes]
-            + [pltpu.SemaphoreType.DMA((2,))],
+            + [pltpu.SemaphoreType.DMA((3,))],
             compiler_params=pltpu.CompilerParams(vmem_limit_bytes=4 * 2**20),
             name="finished",
         )(row_parts, known, direction, scaled, rows, next_rows)

time: 166 us -> 166 us (level)
  no operation moved by 1% of the time
where the time goes in v9:
time: 166 us
  blocking collectives  159 us (96%)
  Pallas kernels  4.09 us (2%)
    all_to_all x11, blocking collectives, exchanged(): return lax.all_to_all(tiles, axis, split_axis=0, concat_axis=0, tiled=True)  159 us

profile of v9, /device:TPU:1, one launch (start us, length us, event | category | flops | bytes accessed | tf_op | source)
XLA Modules:
  0.0 165.9 jit_solution(12788403435985226052)
XLA Ops:
  0.6 0.7 broadcast_in_dim.24
  1.4 15.4 %all_to_all.55 = bf16[8,8,1024]{2,1,0:T(8,128)(2,1)S(1)} all-to-all(bf16[8,8,1024]{2,1,0:T(8,128)(2,1)S(1)} %broadcast_in_dim.24), channel_id=1, replica_groups=mesh['z'=8,'core'=2,'x'=4,'y'=8] {'y'}, dimensions={0} | all-to-all | bytes 262144 | tf_op jit(solution)/shard_map/all_to_all | solution.py:16
  16.7 0.1 broadcast_in_dim.25
  16.8 0.0 copy-start.1
  16.8 0.0 copy-start.2
  16.8 10.7 %all_to_all.56 = bf16[4,8,8,1024]{3,2,1,0:T(8,128)(2,1)S(1)} all-to-all(bf16[4,8,8,1024]{3,2,1,0:T(8,128)(2,1)S(1)} %broadcast_in_dim.25), channel_id=1, replica_groups=mesh['z'=8,'core'=2,'x'=4,'y'=8] {'x'}, dimensions={0} | all-to-all | bytes 1048576 | tf_op jit(solution)/shard_map/all_to_all | solution.py:16
  27.5 0.0 copy-done.1
  27.5 0.0 copy-done.2
  27.5 0.9 built.1
  28.4 0.0 copy-start
  28.5 21.4 %all_to_all.57 = bf16[16,32,128]{2,1,0:T(8,128)(2,1)S(1)} all-to-all(bf16[16,32,128]{2,1,0:T(8,128)(2,1)S(1)} %bitcast.59), channel_id=1, replica_groups=mesh['z'=8,'core'=2,'x'=4,'y'=8] {'core','z'}, dimensions={0} | all-to-all | bytes 262144 | tf_op jit(solution)/shard_map/all_to_all | solution.py:16
  49.9 11.6 %all_to_all.58 = bf16[16,32,128]{2,1,0:T(8,128)(2,1)S(1)} all-to-all(bf16[16,32,128]{2,1,0:T(8,128)(2,1)S(1)} %broadcast_in_dim.26), channel_id=1, replica_groups=mesh['z'=8,'core'=2,'x'=4,'y'=8] {'core','z'}, dimensions={0} | all-to-all | bytes 262144 | tf_op jit(solution)/shard_map/all_to_all | solution.py:16
  61.4 0.0 copy-done
  61.4 0.9 stepped.2
  62.3 13.7 %all_to_all.59 = bf16[32,17,2,128]{3,2,1,0:T(2,128)(2,1)S(1)} all-to-all(bf16[32,17,2,128]{3,2,1,0:T(2,128)(2,1)S(1)} %bitcast.58), channel_id=1, replica_groups=mesh['z'=8,'core'=2,'x'=4,'y'=8] {'y','x'}, dimensions={0} | all-to-all | bytes 557056 | tf_op jit(solution)/shard_map/all_to_all | solution.py:16
  76.1 0.2 convert_reduce_fusion.1
  76.4 15.5 %all_to_all.60 = bf16[32,32,128]{2,1,0:T(8,128)(2,1)S(1)} all-to-all(bf16[32,32,128]{2,1,0:T(8,128)(2,1)S(1)} %broadcast_in_dim.27), channel_id=1, replica_groups=mesh['z'=8,'core'=2,'x'=4,'y'=8] {'y','x'}, dimensions={0} | all-to-all | bytes 524288 | tf_op jit(solution)/shard_map/all_to_all | solution.py:16
  91.9 0.4 returned.1
  92.3 14.9 %all_to_all.61 = bf16[16,17,2,128]{3,2,1,0:T(2,128)(2,1)S(1)} all-to-all(bf16[16,17,2,128]{3,2,1,0:T(2,128)(2,1)S(1)} %bitcast.54), channel_id=1, replica_groups=mesh['z'=8,'core'=2,'x'=4,'y'=8] {'core','z'}, dimensions={0} | all-to-all | bytes 278528 | tf_op jit(solution)/shard_map/all_to_all | solution.py:16
  107.2 0.1 convert_reduce_fusion.2
  107.4 11.7 %all_to_all.62 = bf16[16,32,128]{2,1,0:T(8,128)(2,1)S(1)} all-to-all(bf16[16,32,128]{2,1,0:T(8,128)(2,1)S(1)} %broadcast_in_dim.28), channel_id=1, replica_groups=mesh['z'=8,'core'=2,'x'=4,'y'=8] {'core','z'}, dimensions={0} | all-to-all | bytes 262144 | tf_op jit(solution)/shard_map/all_to_all | solution.py:16
  119.1 0.9 stepped.3
  120.0 14.1 %all_to_all.63 = bf16[32,18,2,128]{3,2,1,0:T(2,128)(2,1)S(1)} all-to-all(bf16[32,18,2,128]{3,2,1,0:T(2,128)(2,1)S(1)} %bitcast.57), channel_id=1, replica_groups=mesh['z'=8,'core'=2,'x'=4,'y'=8] {'y','x'}, dimensions={0} | all-to-all | bytes 589824 | tf_op jit(solution)/shard_map/all_to_all | solution.py:16
  134.1 0.2 convert_reduce_fusion
  134.5 15.8 %all_to_all.64 = bf16[32,32,128]{2,1,0:T(8,128)(2,1)S(1)} all-to-all(bf16[32,32,128]{2,1,0:T(8,128)(2,1)S(1)} %broadcast_in_dim.29), channel_id=1, replica_groups=mesh['z'=8,'core'=2,'x'=4,'y'=8] {'y','x'}, dimensions={0} | all-to-all | bytes 524288 | tf_op jit(solution)/shard_map/all_to_all | solution.py:16
  150.3 0.2 multiply_reduce_fusion
  150.5 14.4 %all_to_all.65 = f32[16,1,128]{2,1,0:T(1,128)S(1)} all-to-all(f32[16,1,128]{2,1,0:T(1,128)S(1)} %broadcast_in_dim.30), channel_id=1, replica_groups=mesh['z'=8,'core'=2,'x'=4,'y'=8] {'core','z'}, dimensions={0} | all-to-all | bytes 16384 | tf_op jit(solution)/shard_map/all_to_all | solution.py:16
  164.9 1.0 finished.1
  (17 shorter events, 0.2 us)
Async XLA Ops:
  16.8 10.7 %copy-start.1 = (bf16[512,256]{1,0:T(8,128)(2,1)S(1)}, bf16[512,256]{1,0:T(8,128)(2,1)}, u32[]{:S(2)}) copy-start(bf16[512,256]{1,0:T(8,128)(2,1)} %centre_points) | copy-start | bytes 786436
  16.8 10.7 %copy-start.2 = (bf16[1024,128]{1,0:T(8,128)(2,1)S(1)}, bf16[1024,128]{1,0:T(8,128)(2,1)}, u32[]{:S(2)}) copy-start(bf16[1024,128]{1,0:T(8,128)(2,1)} %targets.1) | copy-start | bytes 786436
  28.4 33.0 %copy-start = (bf16[512,512]{1,0:T(8,128)(2,1)S(1)}, bf16[512,512]{1,0:T(8,128)(2,1)}, u32[]{:S(2)}) copy-start(bf16[512,512]{1,0:T(8,128)(2,1)} %precond.3) | copy-start | bytes 1572868
